TPU v7x, 256 devices: a whole 4x4x8 slice. The times are simulated.
256 devices in a mesh: ta: 4 (over y), gz: 4 (over x_hi, core), xy: 16 (over x_lo, z).
Axes of the slice: x: 4 (x_hi: 2, x_lo: 2; x = x_hi * 2 + x_lo), y: 4, z: 8, core: 2. Of those that a mesh axis runs over, the one named last changes fastest.
Arguments:
- links: float32 [4, 2, 3, 3, 4, 64, 512], P(None, None, None, None, 'ta', 'xy', 'gz'), may hold values from -0.72 to 1.72
- guess: float32 [12, 2, 4, 3, 4, 64, 512], P(None, None, None, None, 'ta', 'xy', 'gz'), may hold values from -1.5 to 1.5
- source_sites: int32 [4, 16, 4, 4], P('ta', 'xy', 'gz'), may hold values from 0 to 31, as said below
Outputs:
- solution: float32 [12, 2, 4, 3, 4, 64, 512], P(None, None, None, None, 'ta', 'xy', 'gz')
- residual: float32 [12, 2, 4, 3, 4, 64, 512], P(None, None, None, None, 'ta', 'xy', 'gz')
Inputs may be any that keep to these rules, and one draw needn't show every extreme that they name: `source_sites`: each entry is an offset inside its block: time below 1, y below 4, z below 4, x below 32.
All inputs are finite; a program needn't handle non-finite values.
Results may differ from a plain program's by a relative error of at most 0.00012.
Values sent between devices are 32-bit elements; how exact they have to be, the bound alone decides.
No kernel may reach another device: no remote copies, remote signals or barrier semaphores. Data moves between devices by JAX's collectives and lax.ppermute only.
A program may use at most 128 MiB of HBM per device.

v0:
```python
import jax
import jax.numpy as jnp
import numpy as np
from jax import lax
from jax.experimental import pallas as pl
from jax.experimental.pallas import tpu as pltpu
from jax.sharding import Mesh
from jax.sharding import PartitionSpec as P

LX = 32
HOPPING = 0.12
PAIRS = 6
GZ = ("gh", "gc")


def pauli_blocks():
    sigma_one = np.array([[0, 1], [1, 0]], dtype=complex)
    sigma_two = np.array([[0, -1j], [1j, 0]], dtype=complex)
    sigma_three = np.array([[1, 0], [0, -1]], dtype=complex)
    return [-1j * sigma_one, -1j * sigma_two, -1j * sigma_three, np.eye(2, dtype=complex)]


E_BLOCKS = pauli_blocks()


def roll(value, shift, axis):
    size = value.shape[axis]
    shift = shift % size
    return value if shift == 0 else pltpu.roll(value, shift, axis)


def rows():
    return lax.broadcasted_iota(jnp.int32, (8, 128), 0)


def lanes():
    return lax.broadcasted_iota(jnp.int32, (8, 128), 1)


def add_phase(base, phase, value):
    real, imag = value
    if phase == 1:
        return (base[0] + real, base[1] + imag)
    if phase == -1:
        return (base[0] - real, base[1] - imag)
    if phase == 1j:
        return (base[0] - imag, base[1] + real)
    return (base[0] + imag, base[1] - real)


def load_field(ref, pair):
    base = pair * 24
    return [
        [(ref[base + s * 3 + c], ref[base + 12 + s * 3 + c]) for c in range(3)] for s in range(4)
    ]


def project(field, mu, parity):
    block = E_BLOCKS[mu]
    half = []
    for a in range(2):
        b = int(np.flatnonzero(np.abs(block[a]) > 0.5)[0])
        phase = complex(parity * block[a, b])
        half.append([add_phase(field[a][c], phase, field[2 + b][c]) for c in range(3)])
    return half


def lift(total, half, mu, parity):
    block = E_BLOCKS[mu]
    for a in range(2):
        b = int(np.flatnonzero(np.abs(block[a]) > 0.5)[0])
        phase = complex(parity * np.conj(block[a, b]))
        for c in range(3):
            total[a][c] = add_phase(total[a][c], 1, half[a][c])
            total[2 + b][c] = add_phase(total[2 + b][c], phase, half[a][c])


def load_link(ref, base, stride, mu):
    return [
        [
            (
                ref[base + stride * (mu * 18 + a * 3 + b)],
                ref[base + stride * (mu * 18 + 9 + a * 3 + b)],
            )
            for b in range(3)
        ]
        for a in range(3)
    ]


def times(link, vector):
    out = []
    for a in range(3):
        real = imag = None
        for b in range(3):
            ur, ui = link[a][b]
            vr, vi = vector[b]
            tr = ur * vr - ui * vi
            ti = ur * vi + ui * vr
            real = tr if real is None else real + tr
            imag = ti if imag is None else imag + ti
        out.append((real, imag))
    return out


def times_adjoint(link, vector):
    out = []
    for a in range(3):
        real = imag = None
        for b in range(3):
            ur, ui = link[b][a]
            vr, vi = vector[b]
            tr = ur * vr + ui * vi
            ti = ur * vi - ui * vr
            real = tr if real is None else real + tr
            imag = ti if imag is None else imag + ti
        out.append((real, imag))
    return out


def flat(half):
    return [half[a][c][part] for part in range(2) for a in range(2) for c in range(3)]


def unflat(values):
    return [[(values[a * 3 + c], values[6 + a * 3 + c]) for c in range(3)] for a in range(2)]


def map_half(half, fn):
    return [[(fn(re), fn(im)) for re, im in spin] for spin in half]


def pick4(index, parts):
    return jnp.where(
        index < 2,
        jnp.where(index == 0, parts[0], parts[1]),
        jnp.where(index == 2, parts[2], parts[3]),
    )


def x_ahead(value):
    return jnp.where(lanes() % LX == LX - 1, roll(value, LX - 1, 1), roll(value, -1, 1))


def x_behind(value):
    return jnp.where(lanes() % LX == 0, roll(value, 1 - LX, 1), roll(value, 1, 1))


def make_sends(field, pair, links, sign, outs):
    t_ahead, t_behind, y_ahead, y_behind, z_partner, z_other, *carried = outs
    even = lax.axis_index("gc") == 0
    row4 = rows() % 4
    group = lanes() // LX
    half = flat(project(field, 3, -sign))
    for i in range(12):
        t_ahead[pair * 12 + i] = half[i]
    link = load_link(links, 0, 1, 3)
    half = flat([times_adjoint(link, v) for v in project(field, 3, sign)])
    for i in range(12):
        t_behind[pair * 12 + i] = half[i]
    half = flat(project(field, 1, -sign))
    for q in range(3):
        y_ahead[pair * 3 + q] = pick4(row4, [roll(half[4 * q + j], j, 0) for j in range(4)])
    link = load_link(links, 0, 1, 1)
    half = flat([times_adjoint(link, v) for v in project(field, 1, sign)])
    for i in range(12 if carried else 0):
        carried[0][pair * 12 + i] = half[i]
    for q in range(3):
        y_behind[pair * 3 + q] = pick4(row4, [roll(half[4 * q + j], j - 3, 0) for j in range(4)])
    half = flat(project(field, 2, -sign))
    first = [pick4(group, [roll(half[4 * q + j], LX * j, 1) for j in range(4)]) for q in range(3)]
    link = load_link(links, 0, 1, 2)
    half = flat([times_adjoint(link, v) for v in project(field, 2, sign)])
    for i in range(12 if carried else 0):
        carried[1][pair * 12 + i] = half[i]
    for q in range(3):
        last = pick4(group, [roll(half[4 * q + j], LX * (j - 3), 1) for j in range(4)])
        z_partner[pair * 3 + q] = jnp.where(even, last, first[q])
        z_other[pair * 3 + q] = jnp.where(even, first[q], last)


def apply_wilson(field, pair, links, sign, halos, *carried):
    t_ahead, t_behind, y_ahead, y_behind, z_partner, z_other = halos
    even = lax.axis_index("gc") == 0
    row4 = rows() % 4
    group = lanes() // LX

    def carried_tiles(mu):
        if carried:
            return [carried[mu - 1][pair * 12 + i] for i in range(12)]
        return flat([times_adjoint(link, v) for v in project(field, mu, sign)])

    zero = jnp.zeros((8, 128), jnp.float32)
    total = [[(zero, zero) for _ in range(3)] for _ in range(4)]
    link = load_link(links, 0, 1, 0)
    half = map_half(project(field, 0, -sign), x_ahead)
    lift(total, [times(link, v) for v in half], 0, -sign)
    half = [times_adjoint(link, v) for v in project(field, 0, sign)]
    lift(total, map_half(half, x_behind), 0, sign)
    link = load_link(links, 0, 1, 1)
    half = flat(project(field, 1, -sign))
    packed = [y_ahead[pair * 3 + q] for q in range(3)]
    half = [
        jnp.where(row4 == 3, roll(packed[i // 4], 3 - i % 4, 0), roll(half[i], -1, 0))
        for i in range(12)
    ]
    lift(total, [times(link, v) for v in unflat(half)], 1, -sign)
    packed = [y_behind[pair * 3 + q] for q in range(3)]
    own = carried_tiles(1)
    half = [
        jnp.where(row4 == 0, roll(packed[i // 4], -(i % 4), 0), roll(own[i], 1, 0))
        for i in range(12)
    ]
    lift(total, unflat(half), 1, sign)
    link = load_link(links, 0, 1, 2)
    half = flat(project(field, 2, -sign))
    packed = [
        jnp.where(even, z_partner[pair * 3 + q], z_other[pair * 3 + q]) for q in range(3)
    ]
    half = [
        jnp.where(group == 3, roll(packed[i // 4], LX * (3 - i % 4), 1), roll(half[i], -LX, 1))
        for i in range(12)
    ]
    lift(total, [times(link, v) for v in unflat(half)], 2, -sign)
    packed = [
        jnp.where(even, z_other[pair * 3 + q], z_partner[pair * 3 + q]) for q in range(3)
    ]
    own = carried_tiles(2)
    half = [
        jnp.where(group == 0, roll(packed[i // 4], -LX * (i % 4), 1), roll(own[i], LX, 1))
        for i in range(12)
    ]
    lift(total, unflat(half), 2, sign)
    link = load_link(links, 0, 1, 3)
    half = unflat([t_ahead[pair * 12 + i] for i in range(12)])
    lift(total, [times(link, v) for v in half], 3, -sign)
    half = unflat([t_behind[pair * 12 + i] for i in range(12)])
    lift(total, half, 3, sign)
    return [
        [
            tuple(field[s][c][k] - HOPPING * total[s][c][k] for k in range(2))
            for c in range(3)
        ]
        for s in range(4)
    ]


def store_field(ref, pair, field):
    for s in range(4):
        for c in range(3):
            ref[pair * 24 + s * 3 + c] = field[s][c][0]
            ref[pair * 24 + 12 + s * 3 + c] = field[s][c][1]


def norm_row(partials, offset):
    row = rows()
    lane = lanes()
    total = jnp.zeros((8, 128), jnp.float32)
    for pair in range(PAIRS):
        sums = jnp.sum(partials[pair], axis=1, keepdims=True)
        keep = lane == offset + 2 * pair + row // 4
        total = total + jnp.where(keep, sums, 0.0)
    return jnp.sum(total, axis=0, keepdims=True)


def squares(field):
    total = None
    for s in range(4):
        for c in range(3):
            for k in range(2):
                term = field[s][c][k] * field[s][c][k]
                total = term if total is None else total + term
    return total


def block_kernel(source, links, out, sites, link_done, site_done):
    link_copy = pltpu.make_async_copy(links.at[0:216], out.at[0:216], link_done)
    site_copy = pltpu.make_async_copy(source, sites, site_done)
    link_copy.start()
    site_copy.start()
    site_copy.wait()
    hit = (rows() == sites[0, 1]) & (lanes() == sites[0, 2] * LX + sites[0, 3]) & (sites[0, 0] == 0)
    out[216:224] = jnp.where(hit, 1.0, 0.0).astype(jnp.float32)
    link_copy.wait()


def prepare_kernel(last_time, guess, links, field, pair_links, *sends):
    low = rows() < 4
    for k in range(36):
        value = links[8 * k : 8 * k + 8]
        if k >= 27:
            crossing = lax.axis_index("ta") == last_time
            value = jnp.where(crossing, -value, value)
        other = roll(value, 4, 0)
        pair_links[2 * k] = jnp.where(low, value, other)
        pair_links[2 * k + 1] = jnp.where(low, other, value)

    def body(pair, carry):
        for k in range(12):
            start = pl.multiple_of(pair * 192 + 8 * k, 8)
            first = guess[pl.ds(start, 8)]
            second = guess[pl.ds(start + 96, 8)]
            field[pair * 24 + 2 * k] = jnp.where(low, first, roll(second, 4, 0))
            field[pair * 24 + 2 * k + 1] = jnp.where(low, roll(first, 4, 0), second)
        make_sends(load_field(field, pair), pair, pair_links, 1.0, sends)
        return carry

    lax.fori_loop(0, PAIRS, body, 0)


def first_kernel(field, links, ta, tb, ya, yb, za, zb, cy, cz, out):
    def body(pair, carry):
        value = apply_wilson(
            load_field(field, pair), pair, links, 1.0, (ta, tb, ya, yb, za, zb), cy, cz
        )
        store_field(out, pair, value)
        return carry

    lax.fori_loop(0, PAIRS, body, 0)


def defect_kernel(applied, smeared, links, out, *sends):
    low = rows() < 4
    for pair in range(PAIRS):
        spins = [(2 * pair + h) // 3 for h in range(2)]
        colours = [(2 * pair + h) % 3 for h in range(2)]
        for part in range(2):
            for s in range(4):
                for a in range(3):
                    index = pair * 24 + part * 12 + s * 3 + a
                    source = [
                        smeared[colours[h] * 6 + part * 3 + a] if spins[h] == s else 0.0
                        for h in range(2)
                    ]
                    if s in spins:
                        out[index] = jnp.where(low, source[0], source[1]) - applied[index]
                    else:
                        out[index] = -applied[index]

    def body(pair, carry):
        make_sends(load_field(out, pair), pair, links, -1.0, sends)
        return carry

    lax.fori_loop(0, PAIRS, body, 0)


def search_kernel(field, links, ta, tb, ya, yb, za, zb, cy, cz, out, norm, *rest):
    sends, partials = rest[:8], rest[8]

    def body(pair, carry):
        value = apply_wilson(
            load_field(field, pair), pair, links, -1.0, (ta, tb, ya, yb, za, zb), cy, cz
        )
        store_field(out, pair, value)
        partials[pair] = squares(value)
        make_sends(load_field(out, pair), pair, links, 1.0, sends)
        return carry

    lax.fori_loop(0, PAIRS, body, 0)
    norm[...] = jnp.broadcast_to(norm_row([partials[p] for p in range(PAIRS)], 0), (8, 128))


def applied_kernel(field, links, ta, tb, ya, yb, za, zb, cy, cz, norm, out, sums, partials):
    def body(pair, carry):
        value = apply_wilson(
            load_field(field, pair), pair, links, 1.0, (ta, tb, ya, yb, za, zb), cy, cz
        )
        store_field(out, pair, value)
        partials[pair] = squares(value)
        return carry

    lax.fori_loop(0, PAIRS, body, 0)
    row = norm_row([partials[p] for p in range(PAIRS)], 16)
    sums[...] = norm[...] + jnp.broadcast_to(row, (8, 128))


def last_sends_kernel(field, links, *sends):
    def body(pair, carry):
        make_sends(load_field(field, pair), pair, links, -1.0, sends)
        return carry

    lax.fori_loop(0, PAIRS, body, 0)


def stencil_kernel(field, links, ta, tb, ya, yb, za, zb, out):
    def body(pair, carry):
        value = apply_wilson(
            load_field(field, pair), pair, links, -1.0, (ta, tb, ya, yb, za, zb)
        )
        store_field(out, pair, value)
        return carry

    lax.fori_loop(0, PAIRS, body, 0)


def column_sums(ref):
    parts = [ref[8 * k : 8 * k + 8] for k in range(ref.shape[0] // 8)]
    while len(parts) > 1:
        odd = parts[-1:] if len(parts) % 2 else []
        parts = [a + b for a, b in zip(parts[::2], parts[1::2])] + odd
    return jnp.broadcast_to(jnp.sum(parts[0], axis=0, keepdims=True), (8, 128))


def middle_kernel(own, partner, out):
    total = own[...] + partner[...]
    for k in range(out.shape[0] // 8):
        out[8 * k : 8 * k + 8] = total


def columns_kernel(own, far, out):
    out[0:224] = own[...]
    out[224:448] = far[...]


def final_kernel(normal, sums, guess, search, solution, residual, steps):
    low = rows() < 4
    lane = lanes()
    total = column_sums(sums)
    curvature = jnp.where(lane < 12, roll(total, -16, 1), 1.0)
    ratio = total / curvature
    for pair in range(PAIRS):
        keep = lane == 2 * pair + rows() // 4
        step = jnp.sum(jnp.where(keep, ratio, 0.0), axis=1, keepdims=True)
        steps[pair] = jnp.broadcast_to(step, (8, 128))

    def body(pair, carry):
        value = load_field(normal, pair)
        step = steps[pair]
        direction = load_field(search, pair)
        residue = [None] * 24
        update = [None] * 24
        for s in range(4):
            for c in range(3):
                for k in range(2):
                    index = k * 12 + s * 3 + c
                    residue[index] = direction[s][c][k] - step * value[s][c][k]
                    update[index] = step * direction[s][c][k]
        for k in range(12):
            start = pl.multiple_of(pair * 192 + 8 * k, 8)
            even, odd = residue[2 * k], residue[2 * k + 1]
            residual[pl.ds(start, 8)] = jnp.where(low, even, roll(odd, 4, 0))
            residual[pl.ds(start + 96, 8)] = jnp.where(low, roll(even, 4, 0), odd)
            even, odd = update[2 * k], update[2 * k + 1]
            solution[pl.ds(start, 8)] = guess[pl.ds(start, 8)] + jnp.where(
                low, even, roll(odd, 4, 0)
            )
            solution[pl.ds(start + 96, 8)] = guess[pl.ds(start + 96, 8)] + jnp.where(
                low, roll(even, 4, 0), odd
            )
        return carry

    lax.fori_loop(0, PAIRS, body, 0)


def gather_rows(own, below, above):
    row = rows()
    inside = (row >= 2) & (row < 6)
    out = []
    for odd in range(2):
        shift = 6 if odd else 2
        o = roll(own, shift, 0)
        lo = roll(below, 8 - shift, 0)
        hi = roll(above, 8 - shift, 0)
        tile_a = jnp.where(inside, o, jnp.where(row < 2, lo, hi))
        tile_b = jnp.where(row < 4, hi, lo)
        out.append((tile_a, tile_b))
    return out


def colour_field(ref, base, colour):
    return [(ref[base + colour * 6 + a], ref[base + colour * 6 + 3 + a]) for a in range(3)]


def store_colour(ref, base, colour, value):
    for a in range(3):
        ref[base + colour * 6 + a] = value[a][0]
        ref[base + colour * 6 + 3 + a] = value[a][1]


def map_colour(value, fn):
    return [(fn(re), fn(im)) for re, im in value]


def zip_colour(first, second, fn):
    return [(fn(a[0], b[0]), fn(a[1], b[1])) for a, b in zip(first, second)]


def nearest(i):
    return i + (i >> 1)


def four_columns(i):
    return i


def ahead_rows(first, second):
    return jnp.where(rows() == 7, roll(second, -1, 0), roll(first, -1, 0))


def behind_rows(first, second):
    return jnp.where(rows() == 0, roll(second, 1, 0), roll(first, 1, 0))


def ahead_columns(first, second):
    return jnp.where(lanes() < 96, roll(first, -LX, 1), roll(second, -LX, 1))


def behind_columns(first, second):
    return jnp.where(lanes() >= LX, roll(first, LX, 1), roll(second, LX, 1))


def add_colour(first, second):
    return zip_colour(first, second, lambda a, b: a + b)


def next_field(value, total):
    return zip_colour(value, total, lambda a, b: (a + 0.25 * b) * 0.5)


def point_iteration(links_a, links_b, mask_a, mask_b, dst_a, dst_b):
    def update(column, carry):
        base = column * 54
        behind_column = (column + 3) & 3
        ahead_column = (column + 1) & 3
        here_a, here_b = mask_a[column], mask_b[column]

        def conjugate(links, where, mu, colour, mask):
            link = load_link(links, where * 54, 1, mu)
            return [(link[colour][a][0] * mask, -link[colour][a][1] * mask) for a in range(3)]

        for links, dst, mask, other_mask, others in (
            (links_a, dst_a, here_a, here_b, links_b),
            (links_b, dst_b, here_b, here_a, links_a),
        ):
            masks = mask_a if dst is dst_a else mask_b
            shifted = [
                x_ahead(mask),
                ahead_rows(mask, other_mask),
                ahead_columns(mask, masks[ahead_column]),
            ]
            for colour in range(3):
                total = [
                    (shifted[0] * re, shifted[0] * im)
                    for re, im in (row[colour] for row in load_link(links, base, 1, 0))
                ]
                for mu in (1, 2):
                    link = load_link(links, base, 1, mu)
                    total = add_colour(
                        total,
                        [(shifted[mu] * r[colour][0], shifted[mu] * r[colour][1]) for r in link],
                    )
                product = conjugate(links, column, 0, colour, mask)
                total = add_colour(total, map_colour(product, x_behind))
                product = conjugate(links, column, 1, colour, mask)
                other = conjugate(others, column, 1, colour, other_mask)
                total = add_colour(total, zip_colour(product, other, behind_rows))
                product = conjugate(links, column, 2, colour, mask)
                other = conjugate(links, behind_column, 2, colour, masks[behind_column])
                total = add_colour(total, zip_colour(product, other, behind_columns))
                zero = jnp.zeros((8, 128), jnp.float32)
                value = [(mask if a == colour else zero, zero) for a in range(3)]
                store_colour(dst, column * 18, colour, next_field(value, total))
        return carry

    lax.fori_loop(0, 4, update, 0)


def smear_iteration(
    links_a, links_b, src_a, src_b, dst_a, dst_b, carried_a, carried_b, rims, carries, updates
):
    def carry_z(i, carry):
        column = carries[1](i)
        jobs = [(links_a, src_a, carried_a)] + [(links_b, src_b, carried_b)] * (rims == 2)
        for links, src, carried in jobs:
            link = load_link(links, column * 54, 1, 2)
            for colour in range(3):
                value = times_adjoint(link, colour_field(src, column * 18, colour))
                store_colour(carried, column * 18, colour, value)
        return carry

    lax.fori_loop(0, carries[0], carry_z, 0)

    def update(i, carry):
        column = updates[1](i)
        base = column * 54
        here = column * 18
        ahead_column = ((column + 1) & 3) * 18
        behind_column = ((column + 3) & 3) * 18

        def z_part(links, src, carried, colour):
            link = load_link(links, base, 1, 2)
            ahead = zip_colour(
                colour_field(src, here, colour),
                colour_field(src, ahead_column, colour),
                ahead_columns,
            )
            behind = zip_colour(
                colour_field(carried, here, colour),
                colour_field(carried, behind_column, colour),
                behind_columns,
            )
            return add_colour(times(link, ahead), behind)

        def x_part(links, src, colour):
            link = load_link(links, base, 1, 0)
            value = colour_field(src, here, colour)
            ahead = times(link, map_colour(value, x_ahead))
            return add_colour(ahead, map_colour(times_adjoint(link, value), x_behind))

        def y_parts(colour):
            link_a = load_link(links_a, base, 1, 1)
            value_a = colour_field(src_a, here, colour)
            product_a = times_adjoint(link_a, value_a)
            if rims == 0:
                ahead_a = times(link_a, map_colour(value_a, lambda v: roll(v, -1, 0)))
                return [add_colour(ahead_a, map_colour(product_a, lambda v: roll(v, 1, 0)))]
            link_b = load_link(links_b, base, 1, 1)
            value_b = colour_field(src_b, here, colour)
            product_b = times_adjoint(link_b, value_b)
            parts = [
                add_colour(
                    times(link_a, zip_colour(value_a, value_b, ahead_rows)),
                    zip_colour(product_a, product_b, behind_rows),
                )
            ]
            if rims == 2:
                parts.append(
                    add_colour(
                        times(link_b, zip_colour(value_b, value_a, ahead_rows)),
                        zip_colour(product_b, product_a, behind_rows),
                    )
                )
            return parts

        for colour in range(3):
            jobs = [(links_a, src_a, carried_a, dst_a), (links_b, src_b, carried_b, dst_b)]
            for (links, src, carried, dst), y_part in zip(jobs, y_parts(colour)):
                total = add_colour(x_part(links, src, colour), y_part)
                total = add_colour(total, z_part(links, src, carried, colour))
                store_colour(
                    dst, here, colour, next_field(colour_field(src, here, colour), total)
                )
        return carry

    lax.fori_loop(0, updates[0], update, 0)


def smear_first_kernel(
    own, own_p, below, below_p, above, above_p, links_a, links_b, out,
    mask_a, mask_b, fa, fb, ga, gb, ca, cb,
):
    low = rows() < 4
    even = lax.axis_index("gc") == 0

    def build(block, carry):
        for mine, down, up, column in (
            (own, below, above, 2 * block),
            (own_p, below_p, above_p, jnp.where(even, 2 * block + 1, 3 - 2 * block)),
        ):
            for k in range(28):
                start = pl.multiple_of(block * 224 + 8 * k, 8)
                tiles = gather_rows(
                    mine[pl.ds(start, 8)], down[pl.ds(start, 8)], up[pl.ds(start, 8)]
                )
                if k < 27:
                    for odd in range(2):
                        links_a[column * 54 + 2 * k + odd] = tiles[odd][0]
                        links_b[column * 54 + 2 * k + odd] = tiles[odd][1]
            mask_a[column], mask_b[column] = tiles[0]
        return carry

    lax.fori_loop(0, 2, build, 0)
    every, near = (4, four_columns), (3, nearest)
    point_iteration(links_a, links_b, mask_a, mask_b, ga, gb)
    smear_iteration(links_a, links_b, ga, gb, fa, fb, ca, cb, 1, every, every)
    smear_iteration(links_a, links_b, fa, fb, ga, gb, ca, cb, 0, every, every)
    smear_iteration(links_a, links_b, ga, gb, fa, fb, ca, cb, 0, every, near)

    def pack(i, carry):
        column = nearest(i)
        for k in range(9):
            even = roll(fa[column * 18 + 2 * k], 6, 0)
            odd = roll(fa[column * 18 + 2 * k + 1], 2, 0)
            out[i * 9 + k] = jnp.where(low, even, odd)
        return carry

    lax.fori_loop(0, 3, pack, 0)


def smear_second_kernel(links_a, links_b, own, below, above, out, fa, fb, ga, gb, ca, cb):
    low = rows() < 4

    def build(i, carry):
        column = nearest(i)
        for k in range(9):
            index = i * 9 + k
            tiles = gather_rows(own[index], below[index], above[index])
            for odd in range(2):
                fa[column * 18 + 2 * k + odd] = tiles[odd][0]
                fb[column * 18 + 2 * k + odd] = tiles[odd][1]
        return carry

    lax.fori_loop(0, 3, build, 0)
    near, pair, one = (3, nearest), (2, lambda i: 3 * i), (1, four_columns)
    smear_iteration(links_a, links_b, fa, fb, ga, gb, ca, cb, 2, near, near)
    smear_iteration(links_a, links_b, ga, gb, fa, fb, ca, cb, 1, near, near)
    smear_iteration(links_a, links_b, fa, fb, ga, gb, ca, cb, 0, near, near)
    smear_iteration(links_a, links_b, ga, gb, fa, fb, ca, cb, 0, pair, one)
    for i in range(18):
        out[i] = jnp.where(low, roll(fa[i], 6, 0), roll(fa[i], 2, 0))


def call(kernel, outs, args, scratch=(), flops=0):
    vmem = pl.BlockSpec(memory_space=pltpu.VMEM)
    return pl.pallas_call(
        kernel,
        out_shape=[jax.ShapeDtypeStruct(shape, jnp.float32) for shape in outs],
        in_specs=[vmem] * len(args),
        out_specs=[vmem] * len(outs),
        scratch_shapes=[pltpu.VMEM(shape, jnp.float32) for shape in scratch],
        compiler_params=pltpu.CompilerParams(vmem_limit_bytes=12 << 20),
        cost_estimate=pl.CostEstimate(flops=flops, bytes_accessed=0, transcendentals=0),
    )(*args)


def shift(value, axis, amount):
    n = lax.axis_size(axis)
    return lax.ppermute(value, axis, [(i, (i + amount) % n) for i in range(n)])


FULL = (144, 8, 128)
HALF = (72, 8, 128)
RIM = (18, 8, 128)
SENDS = [HALF, HALF, RIM, RIM, RIM, RIM, HALF, HALF]


def swap(value, axis, offset=0):
    n = lax.axis_size(axis)
    pairs = [((i + offset) % n, (i + 1 + offset) % n) for i in range(0, n, 2)]
    return lax.ppermute(value, axis, pairs + [(j, i) for i, j in pairs])


def exchange(sends):
    ta, tb, ya, yb, zp, zo, *carried = sends
    times = (shift(ta, "ta", -1), shift(tb, "ta", 1))
    spaces = (shift(ya, "xy", -1), shift(yb, "xy", 1), swap(zp, "gc"), swap(zo, GZ, 1))
    return (*times, *spaces, *carried)


def whole_step(links, guess, source_sites):
    n_time = lax.axis_size("ta")
    reduced = ("ta", "gh", "xy")
    link_rows = links.reshape(288, 128)
    guess_rows = guess.reshape(1152, 128)

    block = pl.pallas_call(
        block_kernel,
        name="block",
        out_shape=jax.ShapeDtypeStruct((224, 128), jnp.float32),
        in_specs=[pl.BlockSpec(memory_space=pltpu.MemorySpace.HBM)] * 2,
        out_specs=pl.BlockSpec(memory_space=pltpu.VMEM),
        scratch_shapes=[pltpu.SMEM((1, 4), jnp.int32)] + [pltpu.SemaphoreType.DMA] * 2,
        compiler_params=pltpu.CompilerParams(vmem_limit_bytes=12 << 20),
    )(source_sites.reshape(1, 4), link_rows)
    far = swap(block, "gh")
    (own,) = call(columns_kernel, [(448, 128)], (block, far))
    below, above = shift(own, "xy", 1), shift(own, "xy", -1)
    own_p = swap(own, "gc")
    below_p, above_p = swap(below, "gc"), swap(above, "gc")

    def prepare(*refs):
        prepare_kernel(n_time - 1, *refs)

    field, pair_links, *sends = call(
        prepare, [FULL, HALF] + SENDS, (guess_rows, link_rows), flops=4000000
    )
    halos = exchange(sends)
    (applied,) = call(first_kernel, [FULL], (field, pair_links, *halos), flops=8000000)

    tiles = [(72, 8, 128)] * 6
    links_a, links_b, smeared = call(
        smear_first_kernel,
        [(216, 8, 128), (216, 8, 128), (27, 8, 128)],
        (own, own_p, below, below_p, above, above_p),
        scratch=[(4, 8, 128)] * 2 + tiles,
        flops=30000000,
    )
    below, above = shift(smeared, "xy", 1), shift(smeared, "xy", -1)
    (smeared,) = call(
        smear_second_kernel,
        [(18, 8, 128)],
        (links_a, links_b, smeared, below, above),
        scratch=tiles,
        flops=30000000,
    )
    defect, *sends = call(
        defect_kernel, [FULL] + SENDS, (applied, smeared, pair_links), flops=4000000
    )
    search, norm, *sends = call(
        search_kernel,
        [FULL, (8, 128)] + SENDS,
        (defect, pair_links, *exchange(sends)),
        scratch=[(PAIRS, 8, 128)],
        flops=12000000,
    )
    applied, sums = call(
        applied_kernel,
        [FULL, (8, 128)],
        (search, pair_links, *exchange(sends), norm),
        scratch=[(PAIRS, 8, 128)],
        flops=12000000,
    )
    partner = swap(sums, "gc")
    (sums,) = call(middle_kernel, [(lax.axis_size(reduced), 128)], (sums, partner))
    sums = lax.all_to_all(sums, reduced, 0, 0, tiled=True)
    sends = call(last_sends_kernel, SENDS[:6], (applied, pair_links), flops=4000000)
    halos = exchange(sends)
    (normal,) = call(stencil_kernel, [FULL], (applied, pair_links, *halos), flops=8000000)
    solution, residual = call(
        final_kernel,
        [(1152, 128), (1152, 128)],
        (normal, sums, guess_rows, search),
        scratch=[(PAIRS, 8, 128)],
        flops=2000000,
    )
    return solution.reshape(guess.shape), residual.reshape(guess.shape)


def solution(mesh):
    n_time, n_z, n_y = (mesh.shape[axis] for axis in ("ta", "gz", "xy"))
    finer = Mesh(mesh.devices.reshape(n_time, n_z // 2, 2, n_y), ("ta", "gh", "gc", "xy"))
    spec = P(None, None, None, None, "ta", "xy", GZ)
    return jax.shard_map(
        whole_step,
        mesh=finer,
        in_specs=(spec, spec, P("ta", "xy", GZ, None)),
        out_specs=(spec, spec),
        check_vma=False,
    )
```

profile of v0, /device:TPU:1, one launch (start us, length us, event | category | flops | bytes accessed | tf_op | source)
XLA Modules:
  0.0 115.8 jit_solution(12050123828046107802)
XLA Ops:
  0.6 0.0 copy-start.1
  0.7 1.0 copy-done.1
  1.6 0.7 copy-done.3
  2.3 0.7 block.1.own
  3.0 3.6 %collective-permute-start.6 = (f32[224,128]{1,0:T(8,128)S(1)}, f32[224,128]{1,0:T(8,128)S(1)}, u32[]{:S(2)}, u32[]{:S(2)}) collective-permute-start(f32[224,128]{1,0:T(8,128)S(1)} %block.1.own), channel_id=1, source_target_pairs={{0,32},{32,0},{1,33},{33,1},{2,34},{34,2},{3,35},{35,3},{4,36},{36... | collective-permute-start | bytes 344072 | tf_op jit(solution)/shard_map/ppermute | solution.py:740
  6.6 2.2 %collective-permute-done.6.far = f32[224,128]{1,0:T(8,128)S(1)} collective-permute-done((f32[224,128]{1,0:T(8,128)S(1)}, f32[224,128]{1,0:T(8,128)S(1)}, u32[]{:S(2)}, u32[]{:S(2)}) %collective-permute-start.6) | collective-permute-done | bytes 114720 | tf_op jit(solution)/shard_map/ppermute | solution.py:740
  8.8 7.2 %collective-permute-start.10 = (f32[448,128]{1,0:T(8,128)S(1)}, f32[448,128]{1,0:T(8,128)S(1)}, u32[]{:S(2)}, u32[]{:S(2)}) collective-permute-start(f32[448,128]{1,0:T(8,128)S(1)} %shard_map.52.own), channel_id=1, source_target_pairs={{0,15},{1,0},{2,1},{3,2},{4,3},{5,4},{6,5},{7,6},{8,7},{9,8},{10,9... | collective-permute-start | bytes 688136 | tf_op jit(solution)/shard_map/ppermute | solution.py:728
  16.0 1.8 %collective-permute-start.7 = (f32[448,128]{1,0:T(8,128)S(1)}, f32[448,128]{1,0:T(8,128)S(1)}, u32[]{:S(2)}, u32[]{:S(2)}) collective-permute-start(f32[448,128]{1,0:T(8,128)S(1)} %shard_map.52.own), channel_id=1, source_target_pairs={{0,16},{16,0},{1,17},{17,1},{2,18},{18,2},{3,19},{19,3},{4,20},{20... | collective-permute-start | bytes 688136 | tf_op jit(solution)/shard_map/ppermute | solution.py:740
  17.8 1.6 %collective-permute-done.10.above = f32[448,128]{1,0:T(8,128)S(1)} collective-permute-done((f32[448,128]{1,0:T(8,128)S(1)}, f32[448,128]{1,0:T(8,128)S(1)}, u32[]{:S(2)}, u32[]{:S(2)}) %collective-permute-start.10) | collective-permute-done | bytes 229408 | tf_op jit(solution)/shard_map/ppermute | solution.py:728
  19.4 2.4 %collective-permute-start.11 = (f32[448,128]{1,0:T(8,128)S(1)}, f32[448,128]{1,0:T(8,128)S(1)}, u32[]{:S(2)}, u32[]{:S(2)}) collective-permute-start(f32[448,128]{1,0:T(8,128)S(1)} %collective-permute-done.10.above), channel_id=1, source_target_pairs={{0,16},{16,0},{1,17},{17,1},{2,18},{18,2},{3,19},{19,3},{4,20},{20... | collective-permute-start | bytes 688136 | tf_op jit(solution)/shard_map/ppermute | solution.py:740
  21.8 1.6 %collective-permute-done.8.below = f32[448,128]{1,0:T(8,128)S(1)} collective-permute-done((f32[448,128]{1,0:T(8,128)S(1)}, f32[448,128]{1,0:T(8,128)S(1)}, u32[]{:S(2)}, u32[]{:S(2)}) %collective-permute-start.8) | collective-permute-done | bytes 229408 | tf_op jit(solution)/shard_map/ppermute | solution.py:728
  23.5 2.7 %collective-permute-start.9 = (f32[448,128]{1,0:T(8,128)S(1)}, f32[448,128]{1,0:T(8,128)S(1)}, u32[]{:S(2)}, u32[]{:S(2)}) collective-permute-start(f32[448,128]{1,0:T(8,128)S(1)} %collective-permute-done.8.below), channel_id=1, source_target_pairs={{0,16},{16,0},{1,17},{17,1},{2,18},{18,2},{3,19},{19,3},{4,20},{20... | collective-permute-start | bytes 688136 | tf_op jit(solution)/shard_map/ppermute | solution.py:740
  26.1 0.9 copy-done.2
  27.0 0.8 shard_map.50
  27.9 2.8 %collective-permute-start = (f32[72,8,128]{2,1,0:T(8,128)S(1)}, f32[72,8,128]{2,1,0:T(8,128)S(1)}, u32[]{:S(2)}, u32[]{:S(2)}) collective-permute-start(f32[72,8,128]{2,1,0:T(8,128)S(1)} %get-tuple-element.46), channel_id=1, source_target_pairs={{0,192},{64,0},{128,64},{192,128},{1,193},{65,1},{129,65},{193,129... | collective-permute-start | bytes 884744 | tf_op jit(solution)/shard_map/ppermute | solution.py:728
  30.7 0.0 collective-permute-start.1
  30.7 0.0 collective-permute-start.2
  30.7 1.5 %collective-permute-start.3 = (f32[18,8,128]{2,1,0:T(8,128)S(1)}, f32[18,8,128]{2,1,0:T(8,128)S(1)}, u32[]{:S(2)}, u32[]{:S(2)}) collective-permute-start(f32[18,8,128]{2,1,0:T(8,128)S(1)} %get-tuple-element.49), channel_id=1, source_target_pairs={{0,1},{1,2},{2,3},{3,4},{4,5},{5,6},{6,7},{7,8},{8,9},{9,10},{10,1... | collective-permute-start | bytes 221192 | tf_op jit(solution)/shard_map/ppermute | solution.py:728
  32.2 0.8 collective-permute-start.4
  33.0 4.2 %shard_map.53 = (f32[216,8,128]{2,1,0:T(8,128)S(1)}, f32[216,8,128]{2,1,0:T(8,128)S(1)}, f32[27,8,128]{2,1,0:T(8,128)S(1)}) custom-call(f32[448,128]{1,0:T(8,128)S(1)} %shard_map.52.own, f32[448,128]{1,0:T(8,128)S(1)} %collective-permute-done.7.own_p, f32[448,128]{1,0:T(8,128)S(1)} %collective-permute-done.8.below, ...), custom_call_target="tpu_custom_call" | custom-call | flops 30000000 | tf_op jit(solution)/shard_map/pallas_call | solution.py:715
  37.2 2.7 %collective-permute-start.13 = (f32[27,8,128]{2,1,0:T(8,128)S(1)}, f32[27,8,128]{2,1,0:T(8,128)S(1)}, u32[]{:S(2)}, u32[]{:S(2)}) collective-permute-start(f32[27,8,128]{2,1,0:T(8,128)S(1)} %get-tuple-element.56.own), channel_id=1, source_target_pairs={{0,15},{1,0},{2,1},{3,2},{4,3},{5,4},{6,5},{7,6},{8,7},{9,8},{10,9... | collective-permute-start | bytes 331784 | tf_op jit(solution)/shard_map/ppermute | solution.py:728
  39.9 0.0 collective-permute-done.3.yb
  39.9 0.0 collective-permute-start.12
  39.9 0.0 collective-permute-done.4.za
  40.0 2.9 %collective-permute-start.5 = (f32[18,8,128]{2,1,0:T(8,128)S(1)}, f32[18,8,128]{2,1,0:T(8,128)S(1)}, u32[]{:S(2)}, u32[]{:S(2)}) collective-permute-start(f32[18,8,128]{2,1,0:T(8,128)S(1)} %get-tuple-element.51), channel_id=1, source_target_pairs={{16,32},{48,0},{32,16},{0,48},{17,33},{49,1},{33,17},{1,49},{18,34... | collective-permute-start | bytes 221192 | tf_op jit(solution)/shard_map/ppermute | solution.py:740
  42.8 3.9 %collective-permute-done.5.zb = f32[18,8,128]{2,1,0:T(8,128)S(1)} collective-permute-done((f32[18,8,128]{2,1,0:T(8,128)S(1)}, f32[18,8,128]{2,1,0:T(8,128)S(1)}, u32[]{:S(2)}, u32[]{:S(2)}) %collective-permute-start.5) | collective-permute-done | bytes 73760 | tf_op jit(solution)/shard_map/ppermute | solution.py:740
  46.7 0.0 collective-permute-done.ta
  46.7 0.0 collective-permute-done.1.tb
  46.7 1.1 shard_map.51.applied
  47.9 3.4 %shard_map.54.smeared = f32[18,8,128]{2,1,0:T(8,128)S(1)} custom-call(f32[216,8,128]{2,1,0:T(8,128)S(1)} %get-tuple-element.54.links_a, f32[216,8,128]{2,1,0:T(8,128)S(1)} %get-tuple-element.55.links_b, f32[27,8,128]{2,1,0:T(8,128)S(1)} %get-tuple-element.56.own, f32[27,8,128]{2,1,0:T(8,128)S(1)} %collective-permute-done.12.below, ...), custom_call_target="tpu_custom_call" | custom-call | flops 30000000 | tf_op jit(solution)/shard_map/pallas_call | solution.py:715
  51.3 0.8 shard_map.55
  52.1 3.0 %collective-permute-start.14 = (f32[72,8,128]{2,1,0:T(8,128)S(1)}, f32[72,8,128]{2,1,0:T(8,128)S(1)}, u32[]{:S(2)}, u32[]{:S(2)}) collective-permute-start(f32[72,8,128]{2,1,0:T(8,128)S(1)} %get-tuple-element.58), channel_id=1, source_target_pairs={{0,192},{64,0},{128,64},{192,128},{1,193},{65,1},{129,65},{193,129... | collective-permute-start | bytes 884744 | tf_op jit(solution)/shard_map/ppermute | solution.py:728
  55.1 2.9 %collective-permute-start.16 = (f32[18,8,128]{2,1,0:T(8,128)S(1)}, f32[18,8,128]{2,1,0:T(8,128)S(1)}, u32[]{:S(2)}, u32[]{:S(2)}) collective-permute-start(f32[18,8,128]{2,1,0:T(8,128)S(1)} %get-tuple-element.60), channel_id=1, source_target_pairs={{0,15},{1,0},{2,1},{3,2},{4,3},{5,4},{6,5},{7,6},{8,7},{9,8},{10,9... | collective-permute-start | bytes 221192 | tf_op jit(solution)/shard_map/ppermute | solution.py:728
  58.1 0.0 collective-permute-start.17
  58.1 1.0 collective-permute-start.18
  59.0 0.5 collective-permute-done.16.ya
  59.5 4.3 %collective-permute-start.19 = (f32[18,8,128]{2,1,0:T(8,128)S(1)}, f32[18,8,128]{2,1,0:T(8,128)S(1)}, u32[]{:S(2)}, u32[]{:S(2)}) collective-permute-start(f32[18,8,128]{2,1,0:T(8,128)S(1)} %get-tuple-element.63), channel_id=1, source_target_pairs={{16,32},{48,0},{32,16},{0,48},{17,33},{49,1},{33,17},{1,49},{18,34... | collective-permute-start | bytes 221192 | tf_op jit(solution)/shard_map/ppermute | solution.py:740
  63.8 3.7 %collective-permute-done.19.zb = f32[18,8,128]{2,1,0:T(8,128)S(1)} collective-permute-done((f32[18,8,128]{2,1,0:T(8,128)S(1)}, f32[18,8,128]{2,1,0:T(8,128)S(1)}, u32[]{:S(2)}, u32[]{:S(2)}) %collective-permute-start.19) | collective-permute-done | bytes 73760 | tf_op jit(solution)/shard_map/ppermute | solution.py:740
  67.5 0.0 collective-permute-done.14.ta
  67.5 0.0 collective-permute-done.15.tb
  67.5 2.0 %shard_map.56 = (f32[144,8,128]{2,1,0:T(8,128)S(1)}, f32[8,128]{1,0:T(8,128)S(1)}, f32[72,8,128]{2,1,0:T(8,128)S(1)}, f32[72,8,128]{2,1,0:T(8,128)S(1)}, f32[18,...) custom-call(f32[144,8,128]{2,1,0:T(8,128)S(1)} %get-tuple-element.57, ...), custom_call_target="tpu_custom_call" | custom-call | flops 12000000 | tf_op jit(solution)/shard_map/pallas_call | solution.py:715
  69.4 2.8 %collective-permute-start.20 = (f32[72,8,128]{2,1,0:T(8,128)S(1)}, f32[72,8,128]{2,1,0:T(8,128)S(1)}, u32[]{:S(2)}, u32[]{:S(2)}) collective-permute-start(f32[72,8,128]{2,1,0:T(8,128)S(1)} %get-tuple-element.67), channel_id=1, source_target_pairs={{0,192},{64,0},{128,64},{192,128},{1,193},{65,1},{129,65},{193,129... | collective-permute-start | bytes 884744 | tf_op jit(solution)/shard_map/ppermute | solution.py:728
  72.3 1.7 %collective-permute-start.22 = (f32[18,8,128]{2,1,0:T(8,128)S(1)}, f32[18,8,128]{2,1,0:T(8,128)S(1)}, u32[]{:S(2)}, u32[]{:S(2)}) collective-permute-start(f32[18,8,128]{2,1,0:T(8,128)S(1)} %get-tuple-element.69), channel_id=1, source_target_pairs={{0,15},{1,0},{2,1},{3,2},{4,3},{5,4},{6,5},{7,6},{8,7},{9,8},{10,9... | collective-permute-start | bytes 221192 | tf_op jit(solution)/shard_map/ppermute | solution.py:728
  74.0 2.1 %collective-permute-start.24 = (f32[18,8,128]{2,1,0:T(8,128)S(1)}, f32[18,8,128]{2,1,0:T(8,128)S(1)}, u32[]{:S(2)}, u32[]{:S(2)}) collective-permute-start(f32[18,8,128]{2,1,0:T(8,128)S(1)} %get-tuple-element.71), channel_id=1, source_target_pairs={{0,16},{16,0},{1,17},{17,1},{2,18},{18,2},{3,19},{19,3},{4,20},{20... | collective-permute-start | bytes 221192 | tf_op jit(solution)/shard_map/ppermute | solution.py:740
  76.0 0.0 collective-permute-done.22.ya
  76.1 4.3 %collective-permute-start.25 = (f32[18,8,128]{2,1,0:T(8,128)S(1)}, f32[18,8,128]{2,1,0:T(8,128)S(1)}, u32[]{:S(2)}, u32[]{:S(2)}) collective-permute-start(f32[18,8,128]{2,1,0:T(8,128)S(1)} %get-tuple-element.72), channel_id=1, source_target_pairs={{16,32},{48,0},{32,16},{0,48},{17,33},{49,1},{33,17},{1,49},{18,34... | collective-permute-start | bytes 221192 | tf_op jit(solution)/shard_map/ppermute | solution.py:740
  80.4 0.0 collective-permute-done.23.yb
  80.4 0.0 collective-permute-done.24.za
  80.4 3.7 %collective-permute-done.25.zb = f32[18,8,128]{2,1,0:T(8,128)S(1)} collective-permute-done((f32[18,8,128]{2,1,0:T(8,128)S(1)}, f32[18,8,128]{2,1,0:T(8,128)S(1)}, u32[]{:S(2)}, u32[]{:S(2)}) %collective-permute-start.25) | collective-permute-done | bytes 73760 | tf_op jit(solution)/shard_map/ppermute | solution.py:740
  84.1 1.3 %shard_map.57 = (f32[144,8,128]{2,1,0:T(8,128)S(1)}, f32[8,128]{1,0:T(8,128)S(1)}) custom-call(f32[144,8,128]{2,1,0:T(8,128)S(1)} %get-tuple-element.66.field.search, f32[72,8,128]{2,1,0:T(8,128)S(1)} %get-tuple-element.45.links, f32[72,8,128]{2,1,0:T(8,128)S(1)} %collective-permute-done.20.ta, f32[72,8,128]{2,1,0:T(8,128)S(1)} %collective-permute-done.21.tb, ...), custom_call_target="tpu_custom_call" | custom-call | flops 12000000 | tf_op jit(solution)/shard_map/pallas_call | solution.py:715
  85.3 1.3 %shard_map.58 = (f32[72,8,128]{2,1,0:T(8,128)S(1)}, f32[72,8,128]{2,1,0:T(8,128)S(1)}, f32[18,8,128]{2,1,0:T(8,128)}, f32[18,8,128]{2,1,0:T(8,128)S(1)}, f32[18,...) custom-call(f32[144,8,128]{2,1,0:T(8,128)S(1)} %get-tuple-element.76.field, f32[72,8,128]{2,1,0:T(8,128)S(1)} %get-tuple-element.45.links), custom_call_target="tpu_custom_call" | custom-call | flops 4000000 | tf_op jit(solution)/shard_map/pallas_call | solution.py:715
  86.7 3.0 %collective-permute-start.26 = (f32[72,8,128]{2,1,0:T(8,128)S(1)}, f32[72,8,128]{2,1,0:T(8,128)S(1)}, u32[]{:S(2)}, u32[]{:S(2)}) collective-permute-start(f32[72,8,128]{2,1,0:T(8,128)S(1)} %get-tuple-element.77), channel_id=1, source_target_pairs={{0,192},{64,0},{128,64},{192,128},{1,193},{65,1},{129,65},{193,129... | collective-permute-start | bytes 884744 | tf_op jit(solution)/shard_map/ppermute | solution.py:728
  89.6 1.9 %collective-permute-start.28 = (f32[18,8,128]{2,1,0:T(8,128)}, f32[18,8,128]{2,1,0:T(8,128)S(1)}, u32[]{:S(2)}, u32[]{:S(2)}) collective-permute-start(f32[18,8,128]{2,1,0:T(8,128)} %get-tuple-element.79), channel_id=1, source_target_pairs={{0,15},{1,0},{2,1},{3,2},{4,3},{5,4},{6,5},{7,6},{8,7},{9,8},{10,9... | collective-permute-start | bytes 221192 | tf_op jit(solution)/shard_map/ppermute | solution.py:728
  91.6 2.1 %collective-permute-start.32 = (f32[8,128]{1,0:T(8,128)S(1)}, f32[8,128]{1,0:T(8,128)S(1)}, u32[]{:S(2)}, u32[]{:S(2)}) collective-permute-start(f32[8,128]{1,0:T(8,128)S(1)} %get-tuple-element.83.own), channel_id=1, source_target_pairs={{0,16},{16,0},{1,17},{17,1},{2,18},{18,2},{3,19},{19,3},{4,20},{20... | collective-permute-start | bytes 12296 | tf_op jit(solution)/shard_map/ppermute | solution.py:740
  93.7 0.8 collective-permute-done.32.partner
  94.5 0.6 shard_map.60
  95.1 8.6 %all-to-all-start = ((f32[128,1,128]{2,1,0:T(1,128)}), f32[128,1,128]{2,1,0:T(1,128)S(1)}, u32[]{:S(2)}, u32[]{:S(2)}) async-start(f32[128,1,128]{2,1,0:T(1,128)} %bitcast.4), calls=%async_computation | async-start | bytes 131072 | tf_op jit(solution)/shard_map/all_to_all | solution.py:815
  103.7 0.6 collective-permute-start.29
  104.4 1.2 %collective-permute-start.30 = (f32[18,8,128]{2,1,0:T(8,128)S(1)}, f32[18,8,128]{2,1,0:T(8,128)S(1)}, u32[]{:S(2)}, u32[]{:S(2)}) collective-permute-start(f32[18,8,128]{2,1,0:T(8,128)S(1)} %get-tuple-element.81), channel_id=1, source_target_pairs={{0,16},{16,0},{1,17},{17,1},{2,18},{18,2},{3,19},{19,3},{4,20},{20... | collective-permute-start | bytes 221192 | tf_op jit(solution)/shard_map/ppermute | solution.py:740
  105.6 2.6 %collective-permute-start.31 = (f32[18,8,128]{2,1,0:T(8,128)S(1)}, f32[18,8,128]{2,1,0:T(8,128)S(1)}, u32[]{:S(2)}, u32[]{:S(2)}) collective-permute-start(f32[18,8,128]{2,1,0:T(8,128)S(1)} %get-tuple-element.82), channel_id=1, source_target_pairs={{16,32},{48,0},{32,16},{0,48},{17,33},{49,1},{33,17},{1,49},{18,34... | collective-permute-start | bytes 221192 | tf_op jit(solution)/shard_map/ppermute | solution.py:740
  108.2 2.0 %collective-permute-done.29.yb = f32[18,8,128]{2,1,0:T(8,128)S(1)} collective-permute-done((f32[18,8,128]{2,1,0:T(8,128)}, f32[18,8,128]{2,1,0:T(8,128)S(1)}, u32[]{:S(2)}, u32[]{:S(2)}) %collective-permute-start.29) | collective-permute-done | bytes 73760 | tf_op jit(solution)/shard_map/ppermute | solution.py:728
  110.2 3.0 %collective-permute-done.31.zb = f32[18,8,128]{2,1,0:T(8,128)S(1)} collective-permute-done((f32[18,8,128]{2,1,0:T(8,128)S(1)}, f32[18,8,128]{2,1,0:T(8,128)S(1)}, u32[]{:S(2)}, u32[]{:S(2)}) %collective-permute-start.31) | collective-permute-done | bytes 73760 | tf_op jit(solution)/shard_map/ppermute | solution.py:740
  113.2 1.2 %shard_map.59.normal = f32[144,8,128]{2,1,0:T(8,128)S(1)} custom-call(f32[144,8,128]{2,1,0:T(8,128)S(1)} %get-tuple-element.76.field, f32[72,8,128]{2,1,0:T(8,128)S(1)} %get-tuple-element.45.links, f32[72,8,128]{2,1,0:T(8,128)S(1)} %collective-permute-done.26.ta, f32[72,8,128]{2,1,0:T(8,128)S(1)} %collective-permute-done.27.tb, ...), custom_call_target="tpu_custom_call" | custom-call | flops 8000000 | tf_op jit(solution)/shard_map/pallas_call | solution.py:715
  114.4 1.4 %shard_map.61 = (f32[1152,128]{1,0:T(8,128)}, f32[1152,128]{1,0:T(8,128)}) custom-call(f32[144,8,128]{2,1,0:T(8,128)S(1)} %shard_map.59.normal, f32[128,128]{1,0:T(8,128)S(1)} %bitcast.17, f32[1152,128]{1,0:T(8,128)S(1)} %bitcast.14, f32[144,8,128]{2,1,0:T(8,128)S(1)} %get-tuple-element.66.field.search), custom_call_target="tpu_custom_call" | custom-call | flops 2000000 | tf_op jit(solution)/shard_map/pallas_call | solution.py:715
  (27 shorter events, 0.1 us)
Async XLA Ops:
  0.6 25.5 %copy-start = (f32[12,2,4,3,1,4,128]{6,5,4,3,2,1,0:T(4,128)S(1)}, f32[12,2,4,3,1,4,128]{6,5,4,3,2,1,0:T(4,128)}, u32[]{:S(2)}) copy-start(f32[12,2,4,3,1,4,128]{6,5,4,3,2,1,0:T(4,128)} %param.4) | copy-start | bytes 1769476
  0.6 1.0 copy-start.1
  1.6 0.7 copy-start.3
  3.0 5.8 %collective-permute-start.6 = (f32[224,128]{1,0:T(8,128)S(1)}, f32[224,128]{1,0:T(8,128)S(1)}, u32[]{:S(2)}, u32[]{:S(2)}) collective-permute-start(f32[224,128]{1,0:T(8,128)S(1)} %block.1.own), channel_id=1, source_target_pairs={{0,32},{32,0},{1,33},{33,1},{2,34},{34,2},{3,35},{35,3},{4,36},{36... | collective-permute-start | bytes 344072 | tf_op jit(solution)/shard_map/ppermute | solution.py:740
  8.8 10.6 %collective-permute-start.10 = (f32[448,128]{1,0:T(8,128)S(1)}, f32[448,128]{1,0:T(8,128)S(1)}, u32[]{:S(2)}, u32[]{:S(2)}) collective-permute-start(f32[448,128]{1,0:T(8,128)S(1)} %shard_map.52.own), channel_id=1, source_target_pairs={{0,15},{1,0},{2,1},{3,2},{4,3},{5,4},{6,5},{7,6},{8,7},{9,8},{10,9... | collective-permute-start | bytes 688136 | tf_op jit(solution)/shard_map/ppermute | solution.py:728
  16.0 7.5 %collective-permute-start.8 = (f32[448,128]{1,0:T(8,128)S(1)}, f32[448,128]{1,0:T(8,128)S(1)}, u32[]{:S(2)}, u32[]{:S(2)}) collective-permute-start(f32[448,128]{1,0:T(8,128)S(1)} %shard_map.52.own), channel_id=1, source_target_pairs={{0,1},{1,2},{2,3},{3,4},{4,5},{5,6},{6,7},{7,8},{8,9},{9,10},{10,1... | collective-permute-start | bytes 688136 | tf_op jit(solution)/shard_map/ppermute | solution.py:728
  16.0 14.7 %collective-permute-start.7 = (f32[448,128]{1,0:T(8,128)S(1)}, f32[448,128]{1,0:T(8,128)S(1)}, u32[]{:S(2)}, u32[]{:S(2)}) collective-permute-start(f32[448,128]{1,0:T(8,128)S(1)} %shard_map.52.own), channel_id=1, source_target_pairs={{0,16},{16,0},{1,17},{17,1},{2,18},{18,2},{3,19},{19,3},{4,20},{20... | collective-permute-start | bytes 688136 | tf_op jit(solution)/shard_map/ppermute | solution.py:740
  19.4 11.3 %collective-permute-start.11 = (f32[448,128]{1,0:T(8,128)S(1)}, f32[448,128]{1,0:T(8,128)S(1)}, u32[]{:S(2)}, u32[]{:S(2)}) collective-permute-start(f32[448,128]{1,0:T(8,128)S(1)} %collective-permute-done.10.above), channel_id=1, source_target_pairs={{0,16},{16,0},{1,17},{17,1},{2,18},{18,2},{3,19},{19,3},{4,20},{20... | collective-permute-start | bytes 688136 | tf_op jit(solution)/shard_map/ppermute | solution.py:740
  23.5 8.7 %collective-permute-start.9 = (f32[448,128]{1,0:T(8,128)S(1)}, f32[448,128]{1,0:T(8,128)S(1)}, u32[]{:S(2)}, u32[]{:S(2)}) collective-permute-start(f32[448,128]{1,0:T(8,128)S(1)} %collective-permute-done.8.below), channel_id=1, source_target_pairs={{0,16},{16,0},{1,17},{17,1},{2,18},{18,2},{3,19},{19,3},{4,20},{20... | collective-permute-start | bytes 688136 | tf_op jit(solution)/shard_map/ppermute | solution.py:740
  26.1 0.9 copy-start.2
  27.9 18.8 %collective-permute-start = (f32[72,8,128]{2,1,0:T(8,128)S(1)}, f32[72,8,128]{2,1,0:T(8,128)S(1)}, u32[]{:S(2)}, u32[]{:S(2)}) collective-permute-start(f32[72,8,128]{2,1,0:T(8,128)S(1)} %get-tuple-element.46), channel_id=1, source_target_pairs={{0,192},{64,0},{128,64},{192,128},{1,193},{65,1},{129,65},{193,129... | collective-permute-start | bytes 884744 | tf_op jit(solution)/shard_map/ppermute | solution.py:728
  30.7 16.0 %collective-permute-start.1 = (f32[72,8,128]{2,1,0:T(8,128)S(1)}, f32[72,8,128]{2,1,0:T(8,128)S(1)}, u32[]{:S(2)}, u32[]{:S(2)}) collective-permute-start(f32[72,8,128]{2,1,0:T(8,128)S(1)} %get-tuple-element.47), channel_id=1, source_target_pairs={{0,64},{64,128},{128,192},{192,0},{1,65},{65,129},{129,193},{193,1... | collective-permute-start | bytes 884744 | tf_op jit(solution)/shard_map/ppermute | solution.py:728
  30.7 6.5 %collective-permute-start.2 = (f32[18,8,128]{2,1,0:T(8,128)S(1)}, f32[18,8,128]{2,1,0:T(8,128)S(1)}, u32[]{:S(2)}, u32[]{:S(2)}) collective-permute-start(f32[18,8,128]{2,1,0:T(8,128)S(1)} %get-tuple-element.48), channel_id=1, source_target_pairs={{0,15},{1,0},{2,1},{3,2},{4,3},{5,4},{6,5},{7,6},{8,7},{9,8},{10,9... | collective-permute-start | bytes 221192 | tf_op jit(solution)/shard_map/ppermute | solution.py:728
  30.7 9.2 %collective-permute-start.3 = (f32[18,8,128]{2,1,0:T(8,128)S(1)}, f32[18,8,128]{2,1,0:T(8,128)S(1)}, u32[]{:S(2)}, u32[]{:S(2)}) collective-permute-start(f32[18,8,128]{2,1,0:T(8,128)S(1)} %get-tuple-element.49), channel_id=1, source_target_pairs={{0,1},{1,2},{2,3},{3,4},{4,5},{5,6},{6,7},{7,8},{8,9},{9,10},{10,1... | collective-permute-start | bytes 221192 | tf_op jit(solution)/shard_map/ppermute | solution.py:728
  32.2 7.8 %collective-permute-start.4 = (f32[18,8,128]{2,1,0:T(8,128)S(1)}, f32[18,8,128]{2,1,0:T(8,128)S(1)}, u32[]{:S(2)}, u32[]{:S(2)}) collective-permute-start(f32[18,8,128]{2,1,0:T(8,128)S(1)} %get-tuple-element.50), channel_id=1, source_target_pairs={{0,16},{16,0},{1,17},{17,1},{2,18},{18,2},{3,19},{19,3},{4,20},{20... | collective-permute-start | bytes 221192 | tf_op jit(solution)/shard_map/ppermute | solution.py:740
  37.2 10.6 %collective-permute-start.13 = (f32[27,8,128]{2,1,0:T(8,128)S(1)}, f32[27,8,128]{2,1,0:T(8,128)S(1)}, u32[]{:S(2)}, u32[]{:S(2)}) collective-permute-start(f32[27,8,128]{2,1,0:T(8,128)S(1)} %get-tuple-element.56.own), channel_id=1, source_target_pairs={{0,15},{1,0},{2,1},{3,2},{4,3},{5,4},{6,5},{7,6},{8,7},{9,8},{10,9... | collective-permute-start | bytes 331784 | tf_op jit(solution)/shard_map/ppermute | solution.py:728
  39.9 7.9 %collective-permute-start.12 = (f32[27,8,128]{2,1,0:T(8,128)S(1)}, f32[27,8,128]{2,1,0:T(8,128)S(1)}, u32[]{:S(2)}, u32[]{:S(2)}) collective-permute-start(f32[27,8,128]{2,1,0:T(8,128)S(1)} %get-tuple-element.56.own), channel_id=1, source_target_pairs={{0,1},{1,2},{2,3},{3,4},{4,5},{5,6},{6,7},{7,8},{8,9},{9,10},{10,1... | collective-permute-start | bytes 331784 | tf_op jit(solution)/shard_map/ppermute | solution.py:728
  40.0 6.8 %collective-permute-start.5 = (f32[18,8,128]{2,1,0:T(8,128)S(1)}, f32[18,8,128]{2,1,0:T(8,128)S(1)}, u32[]{:S(2)}, u32[]{:S(2)}) collective-permute-start(f32[18,8,128]{2,1,0:T(8,128)S(1)} %get-tuple-element.51), channel_id=1, source_target_pairs={{16,32},{48,0},{32,16},{0,48},{17,33},{49,1},{33,17},{1,49},{18,34... | collective-permute-start | bytes 221192 | tf_op jit(solution)/shard_map/ppermute | solution.py:740
  52.1 15.3 %collective-permute-start.14 = (f32[72,8,128]{2,1,0:T(8,128)S(1)}, f32[72,8,128]{2,1,0:T(8,128)S(1)}, u32[]{:S(2)}, u32[]{:S(2)}) collective-permute-start(f32[72,8,128]{2,1,0:T(8,128)S(1)} %get-tuple-element.58), channel_id=1, source_target_pairs={{0,192},{64,0},{128,64},{192,128},{1,193},{65,1},{129,65},{193,129... | collective-permute-start | bytes 884744 | tf_op jit(solution)/shard_map/ppermute | solution.py:728
  55.1 12.3 %collective-permute-start.15 = (f32[72,8,128]{2,1,0:T(8,128)S(1)}, f32[72,8,128]{2,1,0:T(8,128)S(1)}, u32[]{:S(2)}, u32[]{:S(2)}) collective-permute-start(f32[72,8,128]{2,1,0:T(8,128)S(1)} %get-tuple-element.59), channel_id=1, source_target_pairs={{0,64},{64,128},{128,192},{192,0},{1,65},{65,129},{129,193},{193,1... | collective-permute-start | bytes 884744 | tf_op jit(solution)/shard_map/ppermute | solution.py:728
  55.1 4.3 %collective-permute-start.16 = (f32[18,8,128]{2,1,0:T(8,128)S(1)}, f32[18,8,128]{2,1,0:T(8,128)S(1)}, u32[]{:S(2)}, u32[]{:S(2)}) collective-permute-start(f32[18,8,128]{2,1,0:T(8,128)S(1)} %get-tuple-element.60), channel_id=1, source_target_pairs={{0,15},{1,0},{2,1},{3,2},{4,3},{5,4},{6,5},{7,6},{8,7},{9,8},{10,9... | collective-permute-start | bytes 221192 | tf_op jit(solution)/shard_map/ppermute | solution.py:728
  58.1 5.7 %collective-permute-start.17 = (f32[18,8,128]{2,1,0:T(8,128)S(1)}, f32[18,8,128]{2,1,0:T(8,128)S(1)}, u32[]{:S(2)}, u32[]{:S(2)}) collective-permute-start(f32[18,8,128]{2,1,0:T(8,128)S(1)} %get-tuple-element.61), channel_id=1, source_target_pairs={{0,1},{1,2},{2,3},{3,4},{4,5},{5,6},{6,7},{7,8},{8,9},{9,10},{10,1... | collective-permute-start | bytes 221192 | tf_op jit(solution)/shard_map/ppermute | solution.py:728
  58.1 5.7 %collective-permute-start.18 = (f32[18,8,128]{2,1,0:T(8,128)S(1)}, f32[18,8,128]{2,1,0:T(8,128)S(1)}, u32[]{:S(2)}, u32[]{:S(2)}) collective-permute-start(f32[18,8,128]{2,1,0:T(8,128)S(1)} %get-tuple-element.62), channel_id=1, source_target_pairs={{0,16},{16,0},{1,17},{17,1},{2,18},{18,2},{3,19},{19,3},{4,20},{20... | collective-permute-start | bytes 221192 | tf_op jit(solution)/shard_map/ppermute | solution.py:740
  59.5 8.0 %collective-permute-start.19 = (f32[18,8,128]{2,1,0:T(8,128)S(1)}, f32[18,8,128]{2,1,0:T(8,128)S(1)}, u32[]{:S(2)}, u32[]{:S(2)}) collective-permute-start(f32[18,8,128]{2,1,0:T(8,128)S(1)} %get-tuple-element.63), channel_id=1, source_target_pairs={{16,32},{48,0},{32,16},{0,48},{17,33},{49,1},{33,17},{1,49},{18,34... | collective-permute-start | bytes 221192 | tf_op jit(solution)/shard_map/ppermute | solution.py:740
  69.4 14.6 %collective-permute-start.20 = (f32[72,8,128]{2,1,0:T(8,128)S(1)}, f32[72,8,128]{2,1,0:T(8,128)S(1)}, u32[]{:S(2)}, u32[]{:S(2)}) collective-permute-start(f32[72,8,128]{2,1,0:T(8,128)S(1)} %get-tuple-element.67), channel_id=1, source_target_pairs={{0,192},{64,0},{128,64},{192,128},{1,193},{65,1},{129,65},{193,129... | collective-permute-start | bytes 884744 | tf_op jit(solution)/shard_map/ppermute | solution.py:728
  72.3 11.8 %collective-permute-start.21 = (f32[72,8,128]{2,1,0:T(8,128)S(1)}, f32[72,8,128]{2,1,0:T(8,128)S(1)}, u32[]{:S(2)}, u32[]{:S(2)}) collective-permute-start(f32[72,8,128]{2,1,0:T(8,128)S(1)} %get-tuple-element.68), channel_id=1, source_target_pairs={{0,64},{64,128},{128,192},{192,0},{1,65},{65,129},{129,193},{193,1... | collective-permute-start | bytes 884744 | tf_op jit(solution)/shard_map/ppermute | solution.py:728
  72.3 3.8 %collective-permute-start.22 = (f32[18,8,128]{2,1,0:T(8,128)S(1)}, f32[18,8,128]{2,1,0:T(8,128)S(1)}, u32[]{:S(2)}, u32[]{:S(2)}) collective-permute-start(f32[18,8,128]{2,1,0:T(8,128)S(1)} %get-tuple-element.69), channel_id=1, source_target_pairs={{0,15},{1,0},{2,1},{3,2},{4,3},{5,4},{6,5},{7,6},{8,7},{9,8},{10,9... | collective-permute-start | bytes 221192 | tf_op jit(solution)/shard_map/ppermute | solution.py:728
  74.0 6.4 %collective-permute-start.23 = (f32[18,8,128]{2,1,0:T(8,128)S(1)}, f32[18,8,128]{2,1,0:T(8,128)S(1)}, u32[]{:S(2)}, u32[]{:S(2)}) collective-permute-start(f32[18,8,128]{2,1,0:T(8,128)S(1)} %get-tuple-element.70), channel_id=1, source_target_pairs={{0,1},{1,2},{2,3},{3,4},{4,5},{5,6},{6,7},{7,8},{8,9},{9,10},{10,1... | collective-permute-start | bytes 221192 | tf_op jit(solution)/shard_map/ppermute | solution.py:728
  74.0 6.4 %collective-permute-start.24 = (f32[18,8,128]{2,1,0:T(8,128)S(1)}, f32[18,8,128]{2,1,0:T(8,128)S(1)}, u32[]{:S(2)}, u32[]{:S(2)}) collective-permute-start(f32[18,8,128]{2,1,0:T(8,128)S(1)} %get-tuple-element.71), channel_id=1, source_target_pairs={{0,16},{16,0},{1,17},{17,1},{2,18},{18,2},{3,19},{19,3},{4,20},{20... | collective-permute-start | bytes 221192 | tf_op jit(solution)/shard_map/ppermute | solution.py:740
  76.1 8.0 %collective-permute-start.25 = (f32[18,8,128]{2,1,0:T(8,128)S(1)}, f32[18,8,128]{2,1,0:T(8,128)S(1)}, u32[]{:S(2)}, u32[]{:S(2)}) collective-permute-start(f32[18,8,128]{2,1,0:T(8,128)S(1)} %get-tuple-element.72), channel_id=1, source_target_pairs={{16,32},{48,0},{32,16},{0,48},{17,33},{49,1},{33,17},{1,49},{18,34... | collective-permute-start | bytes 221192 | tf_op jit(solution)/shard_map/ppermute | solution.py:740
  86.7 3.0 %copy-start.4 = (f32[18,8,128]{2,1,0:T(8,128)}, f32[18,8,128]{2,1,0:T(8,128)S(1)}, u32[]{:S(2)}) copy-start(f32[18,8,128]{2,1,0:T(8,128)S(1)} %get-tuple-element.80) | copy-start | bytes 221188
  86.7 26.5 %collective-permute-start.26 = (f32[72,8,128]{2,1,0:T(8,128)S(1)}, f32[72,8,128]{2,1,0:T(8,128)S(1)}, u32[]{:S(2)}, u32[]{:S(2)}) collective-permute-start(f32[72,8,128]{2,1,0:T(8,128)S(1)} %get-tuple-element.77), channel_id=1, source_target_pairs={{0,192},{64,0},{128,64},{192,128},{1,193},{65,1},{129,65},{193,129... | collective-permute-start | bytes 884744 | tf_op jit(solution)/shard_map/ppermute | solution.py:728
  89.6 23.6 %collective-permute-start.27 = (f32[72,8,128]{2,1,0:T(8,128)S(1)}, f32[72,8,128]{2,1,0:T(8,128)S(1)}, u32[]{:S(2)}, u32[]{:S(2)}) collective-permute-start(f32[72,8,128]{2,1,0:T(8,128)S(1)} %get-tuple-element.78), channel_id=1, source_target_pairs={{0,64},{64,128},{128,192},{192,0},{1,65},{65,129},{129,193},{193,1... | collective-permute-start | bytes 884744 | tf_op jit(solution)/shard_map/ppermute | solution.py:728
  89.6 15.9 %collective-permute-start.28 = (f32[18,8,128]{2,1,0:T(8,128)}, f32[18,8,128]{2,1,0:T(8,128)S(1)}, u32[]{:S(2)}, u32[]{:S(2)}) collective-permute-start(f32[18,8,128]{2,1,0:T(8,128)} %get-tuple-element.79), channel_id=1, source_target_pairs={{0,15},{1,0},{2,1},{3,2},{4,3},{5,4},{6,5},{7,6},{8,7},{9,8},{10,9... | collective-permute-start | bytes 221192 | tf_op jit(solution)/shard_map/ppermute | solution.py:728
  91.6 2.9 %collective-permute-start.32 = (f32[8,128]{1,0:T(8,128)S(1)}, f32[8,128]{1,0:T(8,128)S(1)}, u32[]{:S(2)}, u32[]{:S(2)}) collective-permute-start(f32[8,128]{1,0:T(8,128)S(1)} %get-tuple-element.83.own), channel_id=1, source_target_pairs={{0,16},{16,0},{1,17},{17,1},{2,18},{18,2},{3,19},{19,3},{4,20},{20... | collective-permute-start | bytes 12296 | tf_op jit(solution)/shard_map/ppermute | solution.py:740
  95.1 19.3 %all-to-all-start = ((f32[128,1,128]{2,1,0:T(1,128)}), f32[128,1,128]{2,1,0:T(1,128)S(1)}, u32[]{:S(2)}, u32[]{:S(2)}) async-start(f32[128,1,128]{2,1,0:T(1,128)} %bitcast.4), calls=%async_computation | async-start | bytes 131072 | tf_op jit(solution)/shard_map/all_to_all | solution.py:815
  103.7 6.5 %collective-permute-start.29 = (f32[18,8,128]{2,1,0:T(8,128)}, f32[18,8,128]{2,1,0:T(8,128)S(1)}, u32[]{:S(2)}, u32[]{:S(2)}) collective-permute-start(f32[18,8,128]{2,1,0:T(8,128)} %copy-done.4), channel_id=1, source_target_pairs={{0,1},{1,2},{2,3},{3,4},{4,5},{5,6},{6,7},{7,8},{8,9},{9,10},{10,1... | collective-permute-start | bytes 221192 | tf_op jit(solution)/shard_map/ppermute | solution.py:728
  104.4 5.8 %collective-permute-start.30 = (f32[18,8,128]{2,1,0:T(8,128)S(1)}, f32[18,8,128]{2,1,0:T(8,128)S(1)}, u32[]{:S(2)}, u32[]{:S(2)}) collective-permute-start(f32[18,8,128]{2,1,0:T(8,128)S(1)} %get-tuple-element.81), channel_id=1, source_target_pairs={{0,16},{16,0},{1,17},{17,1},{2,18},{18,2},{3,19},{19,3},{4,20},{20... | collective-permute-start | bytes 221192 | tf_op jit(solution)/shard_map/ppermute | solution.py:740
  105.6 7.6 %collective-permute-start.31 = (f32[18,8,128]{2,1,0:T(8,128)S(1)}, f32[18,8,128]{2,1,0:T(8,128)S(1)}, u32[]{:S(2)}, u32[]{:S(2)}) collective-permute-start(f32[18,8,128]{2,1,0:T(8,128)S(1)} %get-tuple-element.82), channel_id=1, source_target_pairs={{16,32},{48,0},{32,16},{0,48},{17,33},{49,1},{33,17},{1,49},{18,34... | collective-permute-start | bytes 221192 | tf_op jit(solution)/shard_map/ppermute | solution.py:740
where the time goes:
time: 116 us
  starting transfers between devices  70.6 us (61%)
  waiting for transfers between devices  23.1 us (20%)
  Pallas kernels  18.8 us (16%)
  local copies, waits for them, and re-layouts  2.54 us (2%)
    ppermute x13, starting transfers between devices, swap(): return lax.ppermute(value, axis, pairs + [(j, i) for i, j in pairs])  31.7 us
    ppermute x20, starting transfers between devices, shift(): return lax.ppermute(value, axis, [(i, (i + amount) % n) for i in range(n)])  30.2 us
    pallas_call x12, Pallas kernels, call(): pl.pallas_call(kernel, out_shape=[jax.ShapeDtypeStruct(shape, jnp.float32...  18.1 us
    ppermute x13, waiting for transfers between devices, swap(): return lax.ppermute(value, axis, pairs + [(j, i) for i, j in pairs])  17.3 us
    all_to_all x1, starting transfers between devices, whole_step(): sums = lax.all_to_all(sums, reduced, 0, 0, tiled=True)  8.63 us
    ppermute x20, waiting for transfers between devices, shift(): return lax.ppermute(value, axis, [(i, (i + amount) % n) for i in range(n)])  5.78 us
    unnamed x10, local copies, waits for them, and re-layouts  2.54 us
  transfers between devices with their start and end apart: 34, of which 10 were waited for; matrix products, arithmetic and copies ran while one was open for 0% of the time, Pallas kernels for 7%

commit v1 on v0

--- a/solution.py
+++ b/solution.py
@@ -407,15 +407,21 @@
         out[8 * k : 8 * k + 8] = total
 
 
+def column_kernel(sums, out):
+    out[...] = column_sums(sums)
+
+
 def columns_kernel(own, far, out):
     out[0:224] = own[...]
     out[224:448] = far[...]
 
 
-def final_kernel(normal, sums, guess, search, solution, residual, steps):
+def final_kernel(
+    normal, sums, sums_far, guess, search, solution, residual, steps, new_solution, new_residual, done
+):
     low = rows() < 4
     lane = lanes()
-    total = column_sums(sums)
+    total = sums[...] + sums_far[...]
     curvature = jnp.where(lane < 12, roll(total, -16, 1), 1.0)
     ratio = total / curvature
     for pair in range(PAIRS):
@@ -423,33 +429,37 @@
         step = jnp.sum(jnp.where(keep, ratio, 0.0), axis=1, keepdims=True)
         steps[pair] = jnp.broadcast_to(step, (8, 128))
 
+    def copies(pair):
+        span = pl.ds(pl.multiple_of(pair * 192, 8), 192)
+        return (
+            pltpu.make_async_copy(new_solution.at[span], solution.at[span], done.at[0, pair]),
+            pltpu.make_async_copy(new_residual.at[span], residual.at[span], done.at[1, pair]),
+        )
+
     def body(pair, carry):
-        value = load_field(normal, pair)
         step = steps[pair]
-        direction = load_field(search, pair)
-        residue = [None] * 24
-        update = [None] * 24
-        for s in range(4):
-            for c in range(3):
-                for k in range(2):
-                    index = k * 12 + s * 3 + c
-                    residue[index] = direction[s][c][k] - step * value[s][c][k]
-                    update[index] = step * direction[s][c][k]
         for k in range(12):
+            index = pair * 24 + 2 * k
             start = pl.multiple_of(pair * 192 + 8 * k, 8)
-            even, odd = residue[2 * k], residue[2 * k + 1]
-            residual[pl.ds(start, 8)] = jnp.where(low, even, roll(odd, 4, 0))
-            residual[pl.ds(start + 96, 8)] = jnp.where(low, roll(even, 4, 0), odd)
-            even, odd = update[2 * k], update[2 * k + 1]
-            solution[pl.ds(start, 8)] = guess[pl.ds(start, 8)] + jnp.where(
+            even, odd = search[index], search[index + 1]
+            left = even - step * normal[index], odd - step * normal[index + 1]
+            even, odd = step * even, step * odd
+            new_residual[pl.ds(start, 8)] = jnp.where(low, left[0], roll(left[1], 4, 0))
+            new_residual[pl.ds(start + 96, 8)] = jnp.where(low, roll(left[0], 4, 0), left[1])
+            new_solution[pl.ds(start, 8)] = guess[pl.ds(start, 8)] + jnp.where(
                 low, even, roll(odd, 4, 0)
             )
-            solution[pl.ds(start + 96, 8)] = guess[pl.ds(start + 96, 8)] + jnp.where(
+            new_solution[pl.ds(start + 96, 8)] = guess[pl.ds(start + 96, 8)] + jnp.where(
                 low, roll(even, 4, 0), odd
             )
+        for copy in copies(pair):
+            copy.start()
         return carry
 
     lax.fori_loop(0, PAIRS, body, 0)
+    for pair in range(PAIRS):
+        for copy in copies(pair):
+            copy.wait()
 
 
 def gather_rows(own, below, above):
@@ -742,14 +752,14 @@
 
 def exchange(sends):
     ta, tb, ya, yb, zp, zo, *carried = sends
+    spaces = (shift(ya, "xy", -1), shift(yb, "xy", 1), swap(zp, "gc"), swap(zo, GZ, 1))
     times = (shift(ta, "ta", -1), shift(tb, "ta", 1))
-    spaces = (shift(ya, "xy", -1), shift(yb, "xy", 1), swap(zp, "gc"), swap(zo, GZ, 1))
     return (*times, *spaces, *carried)
 
 
 def whole_step(links, guess, source_sites):
     n_time = lax.axis_size("ta")
-    reduced = ("ta", "gh", "xy")
+    reduced = ("ta", "xy")
     link_rows = links.reshape(288, 128)
     guess_rows = guess.reshape(1152, 128)
 
@@ -815,14 +825,22 @@
     sums = lax.all_to_all(sums, reduced, 0, 0, tiled=True)
     sends = call(last_sends_kernel, SENDS[:6], (applied, pair_links), flops=4000000)
     halos = exchange(sends)
+    (sums,) = call(column_kernel, [(8, 128)], (sums,))
+    sums_far = swap(sums, "gh")
     (normal,) = call(stencil_kernel, [FULL], (applied, pair_links, *halos), flops=8000000)
-    solution, residual = call(
+    whole = (1152, 128)
+    vmem, anywhere = (pl.BlockSpec(memory_space=space) for space in (pltpu.VMEM, pl.ANY))
+    solution, residual = pl.pallas_call(
         final_kernel,
-        [(1152, 128), (1152, 128)],
-        (normal, sums, guess_rows, search),
-        scratch=[(PAIRS, 8, 128)],
-        flops=2000000,
-    )
+        name="final",
+        out_shape=[jax.ShapeDtypeStruct(whole, jnp.float32)] * 2,
+        in_specs=[vmem] * 5,
+        out_specs=[anywhere] * 2,
+        scratch_shapes=[pltpu.VMEM((PAIRS, 8, 128), jnp.float32)]
+        + [pltpu.VMEM(whole, jnp.float32)] * 2
+        + [pltpu.SemaphoreType.DMA((2, PAIRS))],
+        compiler_params=pltpu.CompilerParams(vmem_limit_bytes=12 << 20),
+    )(normal, sums, sums_far, guess_rows, search)
     return solution.reshape(guess.shape), residual.reshape(guess.shape)
 
 

time: 116 us -> 121 us (1.043)
  blocking collectives: 0 us -> 17.6 us
  starting transfers between devices: 70.6 us -> 63 us
  waiting for transfers between devices: 23.1 us -> 18.9 us
    all_to_all x0 -> x1, blocking collectives: none -> 17.6 us  [whole_step(): sums = lax.all_to_all(sums, reduced, 0, 0, tiled=True)]
    all_to_all x1 -> x0, starting transfers between devices: 8.63 us -> none  [whole_step(): sums = lax.all_to_all(sums, reduced, 0, 0, tiled=True)]
    pallas_call x12, Pallas kernels: 18.1 us -> 15.9 us  [call(): pl.pallas_call(kernel, out_shape=[jax.ShapeDtypeStruct(shape, jnp.float32...]
    ppermute x13 -> x14, waiting for transfers between devices: 17.3 us -> 15.2 us  [swap(): return lax.ppermute(value, axis, pairs + [(j, i) for i, j in pairs])]
    ppermute x20, waiting for transfers between devices: 5.78 us -> 3.76 us  [shift(): return lax.ppermute(value, axis, [(i, (i + amount) % n) for i in range(n)])]
    ppermute x13 -> x14, starting transfers between devices: 31.7 us -> 33.3 us  [swap(): return lax.ppermute(value, axis, pairs + [(j, i) for i, j in pairs])]
    pallas_call x0 -> x1, Pallas kernels: none -> 1.28 us  [whole_step(): pl.pallas_call(final_kernel, name='final', out_shape=[jax.ShapeDtypeStruc...]
    unnamed x10 -> x8, local copies, waits for them, and re-layouts: 2.54 us -> 2.53 us
  transfers between devices with their start and end apart: 34 -> 34, of which waited for: 10 -> 9; matrix products, arithmetic and copies ran while one was open for 0% -> 0% of each run, Pallas kernels for 7% -> 6%
where the time goes in v1:
time: 121 us
  starting transfers between devices  63 us (52%)
  waiting for transfers between devices  18.9 us (16%)
  Pallas kernels  17.9 us (15%)
  blocking collectives  17.6 us (15%)
  local copies, waits for them, and re-layouts  2.53 us (2%)
    ppermute x14, starting transfers between devices, swap(): return lax.ppermute(value, axis, pairs + [(j, i) for i, j in pairs])  33.3 us
    ppermute x20, starting transfers between devices, shift(): return lax.ppermute(value, axis, [(i, (i + amount) % n) for i in range(n)])  29.6 us
    all_to_all x1, blocking collectives, whole_step(): sums = lax.all_to_all(sums, reduced, 0, 0, tiled=True)  17.6 us
    pallas_call x12, Pallas kernels, call(): pl.pallas_call(kernel, out_shape=[jax.ShapeDtypeStruct(shape, jnp.float32...  15.9 us
    ppermute x14, waiting for transfers between devices, swap(): return lax.ppermute(value, axis, pairs + [(j, i) for i, j in pairs])  15.2 us
    ppermute x20, waiting for transfers between devices, shift(): return lax.ppermute(value, axis, [(i, (i + amount) % n) for i in range(n)])  3.76 us
    unnamed x8, local copies, waits for them, and re-layouts  2.53 us
  transfers between devices with their start and end apart: 34, of which 9 were waited for; matrix products, arithmetic and copies ran while one was open for 0% of the time, Pallas kernels for 6%

profile of v1, /device:TPU:1, one launch (start us, length us, event | category | flops | bytes accessed | tf_op | source)
XLA Modules:
  0.0 120.9 jit_solution(6297245135071251107)
XLA Ops:
  0.6 0.0 copy-start.1
  0.7 1.0 copy-done.1
  1.6 0.7 copy-done.3
  2.3 0.7 block.1.own
  3.0 3.6 %collective-permute-start.6 = (f32[224,128]{1,0:T(8,128)S(1)}, f32[224,128]{1,0:T(8,128)S(1)}, u32[]{:S(2)}, u32[]{:S(2)}) collective-permute-start(f32[224,128]{1,0:T(8,128)S(1)} %block.1.own), channel_id=1, source_target_pairs={{0,32},{32,0},{1,33},{33,1},{2,34},{34,2},{3,35},{35,3},{4,36},{36... | collective-permute-start | bytes 344072 | tf_op jit(solution)/shard_map/ppermute | solution.py:750
  6.6 2.2 %collective-permute-done.6.far = f32[224,128]{1,0:T(8,128)S(1)} collective-permute-done((f32[224,128]{1,0:T(8,128)S(1)}, f32[224,128]{1,0:T(8,128)S(1)}, u32[]{:S(2)}, u32[]{:S(2)}) %collective-permute-start.6) | collective-permute-done | bytes 114720 | tf_op jit(solution)/shard_map/ppermute | solution.py:750
  8.8 7.2 %collective-permute-start.10 = (f32[448,128]{1,0:T(8,128)S(1)}, f32[448,128]{1,0:T(8,128)S(1)}, u32[]{:S(2)}, u32[]{:S(2)}) collective-permute-start(f32[448,128]{1,0:T(8,128)S(1)} %shard_map.52.own), channel_id=1, source_target_pairs={{0,15},{1,0},{2,1},{3,2},{4,3},{5,4},{6,5},{7,6},{8,7},{9,8},{10,9... | collective-permute-start | bytes 688136 | tf_op jit(solution)/shard_map/ppermute | solution.py:738
  16.0 1.8 %collective-permute-start.7 = (f32[448,128]{1,0:T(8,128)S(1)}, f32[448,128]{1,0:T(8,128)S(1)}, u32[]{:S(2)}, u32[]{:S(2)}) collective-permute-start(f32[448,128]{1,0:T(8,128)S(1)} %shard_map.52.own), channel_id=1, source_target_pairs={{0,16},{16,0},{1,17},{17,1},{2,18},{18,2},{3,19},{19,3},{4,20},{20... | collective-permute-start | bytes 688136 | tf_op jit(solution)/shard_map/ppermute | solution.py:750
  17.8 1.6 %collective-permute-done.10.above = f32[448,128]{1,0:T(8,128)S(1)} collective-permute-done((f32[448,128]{1,0:T(8,128)S(1)}, f32[448,128]{1,0:T(8,128)S(1)}, u32[]{:S(2)}, u32[]{:S(2)}) %collective-permute-start.10) | collective-permute-done | bytes 229408 | tf_op jit(solution)/shard_map/ppermute | solution.py:738
  19.4 2.4 %collective-permute-start.11 = (f32[448,128]{1,0:T(8,128)S(1)}, f32[448,128]{1,0:T(8,128)S(1)}, u32[]{:S(2)}, u32[]{:S(2)}) collective-permute-start(f32[448,128]{1,0:T(8,128)S(1)} %collective-permute-done.10.above), channel_id=1, source_target_pairs={{0,16},{16,0},{1,17},{17,1},{2,18},{18,2},{3,19},{19,3},{4,20},{20... | collective-permute-start | bytes 688136 | tf_op jit(solution)/shard_map/ppermute | solution.py:750
  21.8 1.6 %collective-permute-done.8.below = f32[448,128]{1,0:T(8,128)S(1)} collective-permute-done((f32[448,128]{1,0:T(8,128)S(1)}, f32[448,128]{1,0:T(8,128)S(1)}, u32[]{:S(2)}, u32[]{:S(2)}) %collective-permute-start.8) | collective-permute-done | bytes 229408 | tf_op jit(solution)/shard_map/ppermute | solution.py:738
  23.5 2.7 %collective-permute-start.9 = (f32[448,128]{1,0:T(8,128)S(1)}, f32[448,128]{1,0:T(8,128)S(1)}, u32[]{:S(2)}, u32[]{:S(2)}) collective-permute-start(f32[448,128]{1,0:T(8,128)S(1)} %collective-permute-done.8.below), channel_id=1, source_target_pairs={{0,16},{16,0},{1,17},{17,1},{2,18},{18,2},{3,19},{19,3},{4,20},{20... | collective-permute-start | bytes 688136 | tf_op jit(solution)/shard_map/ppermute | solution.py:750
  26.1 0.9 copy-done.2
  27.0 0.9 shard_map.50
  27.9 2.8 %collective-permute-start = (f32[72,8,128]{2,1,0:T(8,128)S(1)}, f32[72,8,128]{2,1,0:T(8,128)S(1)}, u32[]{:S(2)}, u32[]{:S(2)}) collective-permute-start(f32[72,8,128]{2,1,0:T(8,128)S(1)} %get-tuple-element.46), channel_id=1, source_target_pairs={{0,192},{64,0},{128,64},{192,128},{1,193},{65,1},{129,65},{193,129... | collective-permute-start | bytes 884744 | tf_op jit(solution)/shard_map/ppermute | solution.py:738
  30.7 0.0 collective-permute-start.1
  30.7 0.0 collective-permute-done.7.own_p
  30.7 0.0 collective-permute-start.2
  30.7 0.0 collective-permute-done.11.above_p
  30.7 1.5 %collective-permute-start.3 = (f32[18,8,128]{2,1,0:T(8,128)S(1)}, f32[18,8,128]{2,1,0:T(8,128)S(1)}, u32[]{:S(2)}, u32[]{:S(2)}) collective-permute-start(f32[18,8,128]{2,1,0:T(8,128)S(1)} %get-tuple-element.49), channel_id=1, source_target_pairs={{0,1},{1,2},{2,3},{3,4},{4,5},{5,6},{6,7},{7,8},{8,9},{9,10},{10,1... | collective-permute-start | bytes 221192 | tf_op jit(solution)/shard_map/ppermute | solution.py:738
  32.2 0.0 collective-permute-done.9.below_p
  32.2 0.8 collective-permute-start.4
  33.0 4.2 %shard_map.53 = (f32[216,8,128]{2,1,0:T(8,128)S(1)}, f32[216,8,128]{2,1,0:T(8,128)S(1)}, f32[27,8,128]{2,1,0:T(8,128)S(1)}) custom-call(f32[448,128]{1,0:T(8,128)S(1)} %shard_map.52.own, f32[448,128]{1,0:T(8,128)S(1)} %collective-permute-done.7.own_p, f32[448,128]{1,0:T(8,128)S(1)} %collective-permute-done.8.below, ...), custom_call_target="tpu_custom_call" | custom-call | flops 30000000 | tf_op jit(solution)/shard_map/pallas_call | solution.py:725
  37.3 2.7 %collective-permute-start.13 = (f32[27,8,128]{2,1,0:T(8,128)S(1)}, f32[27,8,128]{2,1,0:T(8,128)S(1)}, u32[]{:S(2)}, u32[]{:S(2)}) collective-permute-start(f32[27,8,128]{2,1,0:T(8,128)S(1)} %get-tuple-element.56.own), channel_id=1, source_target_pairs={{0,15},{1,0},{2,1},{3,2},{4,3},{5,4},{6,5},{7,6},{8,7},{9,8},{10,9... | collective-permute-start | bytes 331784 | tf_op jit(solution)/shard_map/ppermute | solution.py:738
  40.0 0.0 collective-permute-done.3.yb
  40.0 0.0 collective-permute-start.12
  40.0 0.0 collective-permute-done.4.za
  40.0 2.9 %collective-permute-start.5 = (f32[18,8,128]{2,1,0:T(8,128)S(1)}, f32[18,8,128]{2,1,0:T(8,128)S(1)}, u32[]{:S(2)}, u32[]{:S(2)}) collective-permute-start(f32[18,8,128]{2,1,0:T(8,128)S(1)} %get-tuple-element.51), channel_id=1, source_target_pairs={{16,32},{48,0},{32,16},{0,48},{17,33},{49,1},{33,17},{1,49},{18,34... | collective-permute-start | bytes 221192 | tf_op jit(solution)/shard_map/ppermute | solution.py:750
  42.9 3.9 %collective-permute-done.5.zb = f32[18,8,128]{2,1,0:T(8,128)S(1)} collective-permute-done((f32[18,8,128]{2,1,0:T(8,128)S(1)}, f32[18,8,128]{2,1,0:T(8,128)S(1)}, u32[]{:S(2)}, u32[]{:S(2)}) %collective-permute-start.5) | collective-permute-done | bytes 73760 | tf_op jit(solution)/shard_map/ppermute | solution.py:750
  46.8 0.0 collective-permute-done.ta
  46.8 0.0 collective-permute-done.1.tb
  46.8 1.1 shard_map.51.applied
  47.9 0.0 collective-permute-done.13.above
  47.9 0.0 collective-permute-done.12.below
  47.9 3.5 %shard_map.54.smeared = f32[18,8,128]{2,1,0:T(8,128)S(1)} custom-call(f32[216,8,128]{2,1,0:T(8,128)S(1)} %get-tuple-element.54.links_a, f32[216,8,128]{2,1,0:T(8,128)S(1)} %get-tuple-element.55.links_b, f32[27,8,128]{2,1,0:T(8,128)S(1)} %get-tuple-element.56.own, f32[27,8,128]{2,1,0:T(8,128)S(1)} %collective-permute-done.12.below, ...), custom_call_target="tpu_custom_call" | custom-call | flops 30000000 | tf_op jit(solution)/shard_map/pallas_call | solution.py:725
  51.4 0.8 shard_map.55
  52.3 3.0 %collective-permute-start.14 = (f32[72,8,128]{2,1,0:T(8,128)S(1)}, f32[72,8,128]{2,1,0:T(8,128)S(1)}, u32[]{:S(2)}, u32[]{:S(2)}) collective-permute-start(f32[72,8,128]{2,1,0:T(8,128)S(1)} %get-tuple-element.58), channel_id=1, source_target_pairs={{0,192},{64,0},{128,64},{192,128},{1,193},{65,1},{129,65},{193,129... | collective-permute-start | bytes 884744 | tf_op jit(solution)/shard_map/ppermute | solution.py:738
  55.3 0.0 collective-permute-start.15
  55.3 2.9 %collective-permute-start.16 = (f32[18,8,128]{2,1,0:T(8,128)S(1)}, f32[18,8,128]{2,1,0:T(8,128)S(1)}, u32[]{:S(2)}, u32[]{:S(2)}) collective-permute-start(f32[18,8,128]{2,1,0:T(8,128)S(1)} %get-tuple-element.60), channel_id=1, source_target_pairs={{0,15},{1,0},{2,1},{3,2},{4,3},{5,4},{6,5},{7,6},{8,7},{9,8},{10,9... | collective-permute-start | bytes 221192 | tf_op jit(solution)/shard_map/ppermute | solution.py:738
  58.2 0.0 collective-permute-start.17
  58.2 1.0 collective-permute-start.18
  59.2 0.5 collective-permute-done.16.ya
  59.6 4.3 %collective-permute-start.19 = (f32[18,8,128]{2,1,0:T(8,128)S(1)}, f32[18,8,128]{2,1,0:T(8,128)S(1)}, u32[]{:S(2)}, u32[]{:S(2)}) collective-permute-start(f32[18,8,128]{2,1,0:T(8,128)S(1)} %get-tuple-element.63), channel_id=1, source_target_pairs={{16,32},{48,0},{32,16},{0,48},{17,33},{49,1},{33,17},{1,49},{18,34... | collective-permute-start | bytes 221192 | tf_op jit(solution)/shard_map/ppermute | solution.py:750
  63.9 0.0 collective-permute-done.18.za
  63.9 3.7 %collective-permute-done.19.zb = f32[18,8,128]{2,1,0:T(8,128)S(1)} collective-permute-done((f32[18,8,128]{2,1,0:T(8,128)S(1)}, f32[18,8,128]{2,1,0:T(8,128)S(1)}, u32[]{:S(2)}, u32[]{:S(2)}) %collective-permute-start.19) | collective-permute-done | bytes 73760 | tf_op jit(solution)/shard_map/ppermute | solution.py:750
  67.6 2.0 %shard_map.56 = (f32[144,8,128]{2,1,0:T(8,128)S(1)}, f32[8,128]{1,0:T(8,128)S(1)}, f32[72,8,128]{2,1,0:T(8,128)S(1)}, f32[72,8,128]{2,1,0:T(8,128)S(1)}, f32[18,...) custom-call(f32[144,8,128]{2,1,0:T(8,128)S(1)} %get-tuple-element.57, ...), custom_call_target="tpu_custom_call" | custom-call | flops 12000000 | tf_op jit(solution)/shard_map/pallas_call | solution.py:725
  69.6 2.8 %collective-permute-start.20 = (f32[72,8,128]{2,1,0:T(8,128)S(1)}, f32[72,8,128]{2,1,0:T(8,128)S(1)}, u32[]{:S(2)}, u32[]{:S(2)}) collective-permute-start(f32[72,8,128]{2,1,0:T(8,128)S(1)} %get-tuple-element.67), channel_id=1, source_target_pairs={{0,192},{64,0},{128,64},{192,128},{1,193},{65,1},{129,65},{193,129... | collective-permute-start | bytes 884744 | tf_op jit(solution)/shard_map/ppermute | solution.py:738
  72.5 1.7 %collective-permute-start.22 = (f32[18,8,128]{2,1,0:T(8,128)S(1)}, f32[18,8,128]{2,1,0:T(8,128)S(1)}, u32[]{:S(2)}, u32[]{:S(2)}) collective-permute-start(f32[18,8,128]{2,1,0:T(8,128)S(1)} %get-tuple-element.69), channel_id=1, source_target_pairs={{0,15},{1,0},{2,1},{3,2},{4,3},{5,4},{6,5},{7,6},{8,7},{9,8},{10,9... | collective-permute-start | bytes 221192 | tf_op jit(solution)/shard_map/ppermute | solution.py:738
  74.2 2.1 %collective-permute-start.24 = (f32[18,8,128]{2,1,0:T(8,128)S(1)}, f32[18,8,128]{2,1,0:T(8,128)S(1)}, u32[]{:S(2)}, u32[]{:S(2)}) collective-permute-start(f32[18,8,128]{2,1,0:T(8,128)S(1)} %get-tuple-element.71), channel_id=1, source_target_pairs={{0,16},{16,0},{1,17},{17,1},{2,18},{18,2},{3,19},{19,3},{4,20},{20... | collective-permute-start | bytes 221192 | tf_op jit(solution)/shard_map/ppermute | solution.py:750
  76.3 4.3 %collective-permute-start.25 = (f32[18,8,128]{2,1,0:T(8,128)S(1)}, f32[18,8,128]{2,1,0:T(8,128)S(1)}, u32[]{:S(2)}, u32[]{:S(2)}) collective-permute-start(f32[18,8,128]{2,1,0:T(8,128)S(1)} %get-tuple-element.72), channel_id=1, source_target_pairs={{16,32},{48,0},{32,16},{0,48},{17,33},{49,1},{33,17},{1,49},{18,34... | collective-permute-start | bytes 221192 | tf_op jit(solution)/shard_map/ppermute | solution.py:750
  80.6 3.7 %collective-permute-done.25.zb = f32[18,8,128]{2,1,0:T(8,128)S(1)} collective-permute-done((f32[18,8,128]{2,1,0:T(8,128)S(1)}, f32[18,8,128]{2,1,0:T(8,128)S(1)}, u32[]{:S(2)}, u32[]{:S(2)}) %collective-permute-start.25) | collective-permute-done | bytes 73760 | tf_op jit(solution)/shard_map/ppermute | solution.py:750
  84.3 1.3 %shard_map.57 = (f32[144,8,128]{2,1,0:T(8,128)S(1)}, f32[8,128]{1,0:T(8,128)S(1)}) custom-call(f32[144,8,128]{2,1,0:T(8,128)S(1)} %get-tuple-element.66.field.search, f32[72,8,128]{2,1,0:T(8,128)S(1)} %get-tuple-element.45.links, f32[72,8,128]{2,1,0:T(8,128)S(1)} %collective-permute-done.20.ta, f32[72,8,128]{2,1,0:T(8,128)S(1)} %collective-permute-done.21.tb, ...), custom_call_target="tpu_custom_call" | custom-call | flops 12000000 | tf_op jit(solution)/shard_map/pallas_call | solution.py:725
  85.6 0.8 shard_map.58
  86.3 3.0 %collective-permute-start.26 = (f32[72,8,128]{2,1,0:T(8,128)S(1)}, f32[72,8,128]{2,1,0:T(8,128)S(1)}, u32[]{:S(2)}, u32[]{:S(2)}) collective-permute-start(f32[72,8,128]{2,1,0:T(8,128)S(1)} %get-tuple-element.77), channel_id=1, source_target_pairs={{0,192},{64,0},{128,64},{192,128},{1,193},{65,1},{129,65},{193,129... | collective-permute-start | bytes 884744 | tf_op jit(solution)/shard_map/ppermute | solution.py:738
  89.4 1.9 %collective-permute-start.28 = (f32[18,8,128]{2,1,0:T(8,128)S(1)}, f32[18,8,128]{2,1,0:T(8,128)S(1)}, u32[]{:S(2)}, u32[]{:S(2)}) collective-permute-start(f32[18,8,128]{2,1,0:T(8,128)S(1)} %get-tuple-element.79), channel_id=1, source_target_pairs={{0,15},{1,0},{2,1},{3,2},{4,3},{5,4},{6,5},{7,6},{8,7},{9,8},{10,9... | collective-permute-start | bytes 221192 | tf_op jit(solution)/shard_map/ppermute | solution.py:738
  91.3 2.1 %collective-permute-start.32 = (f32[8,128]{1,0:T(8,128)S(1)}, f32[8,128]{1,0:T(8,128)S(1)}, u32[]{:S(2)}, u32[]{:S(2)}) collective-permute-start(f32[8,128]{1,0:T(8,128)S(1)} %get-tuple-element.83.own), channel_id=1, source_target_pairs={{0,16},{16,0},{1,17},{17,1},{2,18},{18,2},{3,19},{19,3},{4,20},{20... | collective-permute-start | bytes 12296 | tf_op jit(solution)/shard_map/ppermute | solution.py:750
  93.4 0.8 collective-permute-done.32.partner
  94.2 0.3 collective-permute-start.30
  94.6 3.1 %collective-permute-start.31 = (f32[18,8,128]{2,1,0:T(8,128)S(1)}, f32[18,8,128]{2,1,0:T(8,128)S(1)}, u32[]{:S(2)}, u32[]{:S(2)}) collective-permute-start(f32[18,8,128]{2,1,0:T(8,128)S(1)} %get-tuple-element.82), channel_id=1, source_target_pairs={{16,32},{48,0},{32,16},{0,48},{17,33},{49,1},{33,17},{1,49},{18,34... | collective-permute-start | bytes 221192 | tf_op jit(solution)/shard_map/ppermute | solution.py:750
  97.7 17.6 %all_to_all.11 = f32[64,1,128]{2,1,0:T(1,128)S(1)} all-to-all(f32[64,1,128]{2,1,0:T(1,128)S(1)} %bitcast.17), channel_id=1, replica_groups=mesh['ta'=4,'gh'=2,'gc'=2,'xy'=16] {'ta','xy'}, dimensions={0} | all-to-all | bytes 65536 | tf_op jit(solution)/shard_map/all_to_all | solution.py:825
  115.4 1.9 %collective-permute-start.33 = (f32[8,128]{1,0:T(8,128)S(1)}, f32[8,128]{1,0:T(8,128)S(1)}, u32[]{:S(2)}, u32[]{:S(2)}) collective-permute-start(f32[8,128]{1,0:T(8,128)S(1)} %shard_map.61.sums), channel_id=1, source_target_pairs={{0,32},{32,0},{1,33},{33,1},{2,34},{34,2},{3,35},{35,3},{4,36},{36... | collective-permute-start | bytes 12296 | tf_op jit(solution)/shard_map/ppermute | solution.py:750
  117.3 1.3 %shard_map.59.normal = f32[144,8,128]{2,1,0:T(8,128)S(1)} custom-call(f32[144,8,128]{2,1,0:T(8,128)S(1)} %get-tuple-element.76.field, f32[72,8,128]{2,1,0:T(8,128)S(1)} %get-tuple-element.45.links, f32[72,8,128]{2,1,0:T(8,128)S(1)} %collective-permute-done.26.ta, f32[72,8,128]{2,1,0:T(8,128)S(1)} %collective-permute-done.27.tb, ...), custom_call_target="tpu_custom_call" | custom-call | flops 8000000 | tf_op jit(solution)/shard_map/pallas_call | solution.py:725
  118.5 0.9 collective-permute-done.33.sums_far
  119.4 1.3 %final.1 = (f32[1152,128]{1,0:T(8,128)}, f32[1152,128]{1,0:T(8,128)}) custom-call(f32[144,8,128]{2,1,0:T(8,128)S(1)} %shard_map.59.normal, f32[8,128]{1,0:T(8,128)S(1)} %shard_map.61.sums, f32[8,128]{1,0:T(8,128)S(1)} %collective-permute-done.33.sums_far, f32[1152,128]{1,0:T(8,128)S(1)} %bitcast.14, f32[144,8,128]{2,1,0:T(8,128)S(1)} %get-tuple-element.66.field.search), custom_call_target="tpu_custom_call" | custom-call | tf_op jit(solution)/shard_map/final/pallas_call | solution.py:833
  (27 shorter events, 0.1 us)
Async XLA Ops:
  0.6 25.5 %copy-start = (f32[12,2,4,3,1,4,128]{6,5,4,3,2,1,0:T(4,128)S(1)}, f32[12,2,4,3,1,4,128]{6,5,4,3,2,1,0:T(4,128)}, u32[]{:S(2)}) copy-start(f32[12,2,4,3,1,4,128]{6,5,4,3,2,1,0:T(4,128)} %param.4) | copy-start | bytes 1769476
  0.6 1.0 copy-start.1
  1.6 0.7 copy-start.3
  3.0 5.8 %collective-permute-start.6 = (f32[224,128]{1,0:T(8,128)S(1)}, f32[224,128]{1,0:T(8,128)S(1)}, u32[]{:S(2)}, u32[]{:S(2)}) collective-permute-start(f32[224,128]{1,0:T(8,128)S(1)} %block.1.own), channel_id=1, source_target_pairs={{0,32},{32,0},{1,33},{33,1},{2,34},{34,2},{3,35},{35,3},{4,36},{36... | collective-permute-start | bytes 344072 | tf_op jit(solution)/shard_map/ppermute | solution.py:750
  8.8 10.6 %collective-permute-start.10 = (f32[448,128]{1,0:T(8,128)S(1)}, f32[448,128]{1,0:T(8,128)S(1)}, u32[]{:S(2)}, u32[]{:S(2)}) collective-permute-start(f32[448,128]{1,0:T(8,128)S(1)} %shard_map.52.own), channel_id=1, source_target_pairs={{0,15},{1,0},{2,1},{3,2},{4,3},{5,4},{6,5},{7,6},{8,7},{9,8},{10,9... | collective-permute-start | bytes 688136 | tf_op jit(solution)/shard_map/ppermute | solution.py:738
  16.0 7.5 %collective-permute-start.8 = (f32[448,128]{1,0:T(8,128)S(1)}, f32[448,128]{1,0:T(8,128)S(1)}, u32[]{:S(2)}, u32[]{:S(2)}) collective-permute-start(f32[448,128]{1,0:T(8,128)S(1)} %shard_map.52.own), channel_id=1, source_target_pairs={{0,1},{1,2},{2,3},{3,4},{4,5},{5,6},{6,7},{7,8},{8,9},{9,10},{10,1... | collective-permute-start | bytes 688136 | tf_op jit(solution)/shard_map/ppermute | solution.py:738
  16.0 14.7 %collective-permute-start.7 = (f32[448,128]{1,0:T(8,128)S(1)}, f32[448,128]{1,0:T(8,128)S(1)}, u32[]{:S(2)}, u32[]{:S(2)}) collective-permute-start(f32[448,128]{1,0:T(8,128)S(1)} %shard_map.52.own), channel_id=1, source_target_pairs={{0,16},{16,0},{1,17},{17,1},{2,18},{18,2},{3,19},{19,3},{4,20},{20... | collective-permute-start | bytes 688136 | tf_op jit(solution)/shard_map/ppermute | solution.py:750
  19.4 11.3 %collective-permute-start.11 = (f32[448,128]{1,0:T(8,128)S(1)}, f32[448,128]{1,0:T(8,128)S(1)}, u32[]{:S(2)}, u32[]{:S(2)}) collective-permute-start(f32[448,128]{1,0:T(8,128)S(1)} %collective-permute-done.10.above), channel_id=1, source_target_pairs={{0,16},{16,0},{1,17},{17,1},{2,18},{18,2},{3,19},{19,3},{4,20},{20... | collective-permute-start | bytes 688136 | tf_op jit(solution)/shard_map/ppermute | solution.py:750
  23.5 8.7 %collective-permute-start.9 = (f32[448,128]{1,0:T(8,128)S(1)}, f32[448,128]{1,0:T(8,128)S(1)}, u32[]{:S(2)}, u32[]{:S(2)}) collective-permute-start(f32[448,128]{1,0:T(8,128)S(1)} %collective-permute-done.8.below), channel_id=1, source_target_pairs={{0,16},{16,0},{1,17},{17,1},{2,18},{18,2},{3,19},{19,3},{4,20},{20... | collective-permute-start | bytes 688136 | tf_op jit(solution)/shard_map/ppermute | solution.py:750
  26.1 0.9 copy-start.2
  27.9 18.9 %collective-permute-start = (f32[72,8,128]{2,1,0:T(8,128)S(1)}, f32[72,8,128]{2,1,0:T(8,128)S(1)}, u32[]{:S(2)}, u32[]{:S(2)}) collective-permute-start(f32[72,8,128]{2,1,0:T(8,128)S(1)} %get-tuple-element.46), channel_id=1, source_target_pairs={{0,192},{64,0},{128,64},{192,128},{1,193},{65,1},{129,65},{193,129... | collective-permute-start | bytes 884744 | tf_op jit(solution)/shard_map/ppermute | solution.py:738
  30.7 16.1 %collective-permute-start.1 = (f32[72,8,128]{2,1,0:T(8,128)S(1)}, f32[72,8,128]{2,1,0:T(8,128)S(1)}, u32[]{:S(2)}, u32[]{:S(2)}) collective-permute-start(f32[72,8,128]{2,1,0:T(8,128)S(1)} %get-tuple-element.47), channel_id=1, source_target_pairs={{0,64},{64,128},{128,192},{192,0},{1,65},{65,129},{129,193},{193,1... | collective-permute-start | bytes 884744 | tf_op jit(solution)/shard_map/ppermute | solution.py:738
  30.7 6.6 %collective-permute-start.2 = (f32[18,8,128]{2,1,0:T(8,128)S(1)}, f32[18,8,128]{2,1,0:T(8,128)S(1)}, u32[]{:S(2)}, u32[]{:S(2)}) collective-permute-start(f32[18,8,128]{2,1,0:T(8,128)S(1)} %get-tuple-element.48), channel_id=1, source_target_pairs={{0,15},{1,0},{2,1},{3,2},{4,3},{5,4},{6,5},{7,6},{8,7},{9,8},{10,9... | collective-permute-start | bytes 221192 | tf_op jit(solution)/shard_map/ppermute | solution.py:738
  30.7 9.3 %collective-permute-start.3 = (f32[18,8,128]{2,1,0:T(8,128)S(1)}, f32[18,8,128]{2,1,0:T(8,128)S(1)}, u32[]{:S(2)}, u32[]{:S(2)}) collective-permute-start(f32[18,8,128]{2,1,0:T(8,128)S(1)} %get-tuple-element.49), channel_id=1, source_target_pairs={{0,1},{1,2},{2,3},{3,4},{4,5},{5,6},{6,7},{7,8},{8,9},{9,10},{10,1... | collective-permute-start | bytes 221192 | tf_op jit(solution)/shard_map/ppermute | solution.py:738
  32.2 7.8 %collective-permute-start.4 = (f32[18,8,128]{2,1,0:T(8,128)S(1)}, f32[18,8,128]{2,1,0:T(8,128)S(1)}, u32[]{:S(2)}, u32[]{:S(2)}) collective-permute-start(f32[18,8,128]{2,1,0:T(8,128)S(1)} %get-tuple-element.50), channel_id=1, source_target_pairs={{0,16},{16,0},{1,17},{17,1},{2,18},{18,2},{3,19},{19,3},{4,20},{20... | collective-permute-start | bytes 221192 | tf_op jit(solution)/shard_map/ppermute | solution.py:750
  37.3 10.6 %collective-permute-start.13 = (f32[27,8,128]{2,1,0:T(8,128)S(1)}, f32[27,8,128]{2,1,0:T(8,128)S(1)}, u32[]{:S(2)}, u32[]{:S(2)}) collective-permute-start(f32[27,8,128]{2,1,0:T(8,128)S(1)} %get-tuple-element.56.own), channel_id=1, source_target_pairs={{0,15},{1,0},{2,1},{3,2},{4,3},{5,4},{6,5},{7,6},{8,7},{9,8},{10,9... | collective-permute-start | bytes 331784 | tf_op jit(solution)/shard_map/ppermute | solution.py:738
  40.0 7.9 %collective-permute-start.12 = (f32[27,8,128]{2,1,0:T(8,128)S(1)}, f32[27,8,128]{2,1,0:T(8,128)S(1)}, u32[]{:S(2)}, u32[]{:S(2)}) collective-permute-start(f32[27,8,128]{2,1,0:T(8,128)S(1)} %get-tuple-element.56.own), channel_id=1, source_target_pairs={{0,1},{1,2},{2,3},{3,4},{4,5},{5,6},{6,7},{7,8},{8,9},{9,10},{10,1... | collective-permute-start | bytes 331784 | tf_op jit(solution)/shard_map/ppermute | solution.py:738
  40.0 6.8 %collective-permute-start.5 = (f32[18,8,128]{2,1,0:T(8,128)S(1)}, f32[18,8,128]{2,1,0:T(8,128)S(1)}, u32[]{:S(2)}, u32[]{:S(2)}) collective-permute-start(f32[18,8,128]{2,1,0:T(8,128)S(1)} %get-tuple-element.51), channel_id=1, source_target_pairs={{16,32},{48,0},{32,16},{0,48},{17,33},{49,1},{33,17},{1,49},{18,34... | collective-permute-start | bytes 221192 | tf_op jit(solution)/shard_map/ppermute | solution.py:750
  52.3 15.3 %collective-permute-start.14 = (f32[72,8,128]{2,1,0:T(8,128)S(1)}, f32[72,8,128]{2,1,0:T(8,128)S(1)}, u32[]{:S(2)}, u32[]{:S(2)}) collective-permute-start(f32[72,8,128]{2,1,0:T(8,128)S(1)} %get-tuple-element.58), channel_id=1, source_target_pairs={{0,192},{64,0},{128,64},{192,128},{1,193},{65,1},{129,65},{193,129... | collective-permute-start | bytes 884744 | tf_op jit(solution)/shard_map/ppermute | solution.py:738
  55.3 12.3 %collective-permute-start.15 = (f32[72,8,128]{2,1,0:T(8,128)S(1)}, f32[72,8,128]{2,1,0:T(8,128)S(1)}, u32[]{:S(2)}, u32[]{:S(2)}) collective-permute-start(f32[72,8,128]{2,1,0:T(8,128)S(1)} %get-tuple-element.59), channel_id=1, source_target_pairs={{0,64},{64,128},{128,192},{192,0},{1,65},{65,129},{129,193},{193,1... | collective-permute-start | bytes 884744 | tf_op jit(solution)/shard_map/ppermute | solution.py:738
  55.3 4.3 %collective-permute-start.16 = (f32[18,8,128]{2,1,0:T(8,128)S(1)}, f32[18,8,128]{2,1,0:T(8,128)S(1)}, u32[]{:S(2)}, u32[]{:S(2)}) collective-permute-start(f32[18,8,128]{2,1,0:T(8,128)S(1)} %get-tuple-element.60), channel_id=1, source_target_pairs={{0,15},{1,0},{2,1},{3,2},{4,3},{5,4},{6,5},{7,6},{8,7},{9,8},{10,9... | collective-permute-start | bytes 221192 | tf_op jit(solution)/shard_map/ppermute | solution.py:738
  58.2 5.7 %collective-permute-start.17 = (f32[18,8,128]{2,1,0:T(8,128)S(1)}, f32[18,8,128]{2,1,0:T(8,128)S(1)}, u32[]{:S(2)}, u32[]{:S(2)}) collective-permute-start(f32[18,8,128]{2,1,0:T(8,128)S(1)} %get-tuple-element.61), channel_id=1, source_target_pairs={{0,1},{1,2},{2,3},{3,4},{4,5},{5,6},{6,7},{7,8},{8,9},{9,10},{10,1... | collective-permute-start | bytes 221192 | tf_op jit(solution)/shard_map/ppermute | solution.py:738
  58.2 5.7 %collective-permute-start.18 = (f32[18,8,128]{2,1,0:T(8,128)S(1)}, f32[18,8,128]{2,1,0:T(8,128)S(1)}, u32[]{:S(2)}, u32[]{:S(2)}) collective-permute-start(f32[18,8,128]{2,1,0:T(8,128)S(1)} %get-tuple-element.62), channel_id=1, source_target_pairs={{0,16},{16,0},{1,17},{17,1},{2,18},{18,2},{3,19},{19,3},{4,20},{20... | collective-permute-start | bytes 221192 | tf_op jit(solution)/shard_map/ppermute | solution.py:750
  59.6 8.0 %collective-permute-start.19 = (f32[18,8,128]{2,1,0:T(8,128)S(1)}, f32[18,8,128]{2,1,0:T(8,128)S(1)}, u32[]{:S(2)}, u32[]{:S(2)}) collective-permute-start(f32[18,8,128]{2,1,0:T(8,128)S(1)} %get-tuple-element.63), channel_id=1, source_target_pairs={{16,32},{48,0},{32,16},{0,48},{17,33},{49,1},{33,17},{1,49},{18,34... | collective-permute-start | bytes 221192 | tf_op jit(solution)/shard_map/ppermute | solution.py:750
  69.6 14.6 %collective-permute-start.20 = (f32[72,8,128]{2,1,0:T(8,128)S(1)}, f32[72,8,128]{2,1,0:T(8,128)S(1)}, u32[]{:S(2)}, u32[]{:S(2)}) collective-permute-start(f32[72,8,128]{2,1,0:T(8,128)S(1)} %get-tuple-element.67), channel_id=1, source_target_pairs={{0,192},{64,0},{128,64},{192,128},{1,193},{65,1},{129,65},{193,129... | collective-permute-start | bytes 884744 | tf_op jit(solution)/shard_map/ppermute | solution.py:738
  72.4 11.8 %collective-permute-start.21 = (f32[72,8,128]{2,1,0:T(8,128)S(1)}, f32[72,8,128]{2,1,0:T(8,128)S(1)}, u32[]{:S(2)}, u32[]{:S(2)}) collective-permute-start(f32[72,8,128]{2,1,0:T(8,128)S(1)} %get-tuple-element.68), channel_id=1, source_target_pairs={{0,64},{64,128},{128,192},{192,0},{1,65},{65,129},{129,193},{193,1... | collective-permute-start | bytes 884744 | tf_op jit(solution)/shard_map/ppermute | solution.py:738
  72.5 3.8 %collective-permute-start.22 = (f32[18,8,128]{2,1,0:T(8,128)S(1)}, f32[18,8,128]{2,1,0:T(8,128)S(1)}, u32[]{:S(2)}, u32[]{:S(2)}) collective-permute-start(f32[18,8,128]{2,1,0:T(8,128)S(1)} %get-tuple-element.69), channel_id=1, source_target_pairs={{0,15},{1,0},{2,1},{3,2},{4,3},{5,4},{6,5},{7,6},{8,7},{9,8},{10,9... | collective-permute-start | bytes 221192 | tf_op jit(solution)/shard_map/ppermute | solution.py:738
  74.2 6.4 %collective-permute-start.23 = (f32[18,8,128]{2,1,0:T(8,128)S(1)}, f32[18,8,128]{2,1,0:T(8,128)S(1)}, u32[]{:S(2)}, u32[]{:S(2)}) collective-permute-start(f32[18,8,128]{2,1,0:T(8,128)S(1)} %get-tuple-element.70), channel_id=1, source_target_pairs={{0,1},{1,2},{2,3},{3,4},{4,5},{5,6},{6,7},{7,8},{8,9},{9,10},{10,1... | collective-permute-start | bytes 221192 | tf_op jit(solution)/shard_map/ppermute | solution.py:738
  74.2 6.4 %collective-permute-start.24 = (f32[18,8,128]{2,1,0:T(8,128)S(1)}, f32[18,8,128]{2,1,0:T(8,128)S(1)}, u32[]{:S(2)}, u32[]{:S(2)}) collective-permute-start(f32[18,8,128]{2,1,0:T(8,128)S(1)} %get-tuple-element.71), channel_id=1, source_target_pairs={{0,16},{16,0},{1,17},{17,1},{2,18},{18,2},{3,19},{19,3},{4,20},{20... | collective-permute-start | bytes 221192 | tf_op jit(solution)/shard_map/ppermute | solution.py:750
  76.3 8.0 %collective-permute-start.25 = (f32[18,8,128]{2,1,0:T(8,128)S(1)}, f32[18,8,128]{2,1,0:T(8,128)S(1)}, u32[]{:S(2)}, u32[]{:S(2)}) collective-permute-start(f32[18,8,128]{2,1,0:T(8,128)S(1)} %get-tuple-element.72), channel_id=1, source_target_pairs={{16,32},{48,0},{32,16},{0,48},{17,33},{49,1},{33,17},{1,49},{18,34... | collective-permute-start | bytes 221192 | tf_op jit(solution)/shard_map/ppermute | solution.py:750
  86.3 30.9 %collective-permute-start.26 = (f32[72,8,128]{2,1,0:T(8,128)S(1)}, f32[72,8,128]{2,1,0:T(8,128)S(1)}, u32[]{:S(2)}, u32[]{:S(2)}) collective-permute-start(f32[72,8,128]{2,1,0:T(8,128)S(1)} %get-tuple-element.77), channel_id=1, source_target_pairs={{0,192},{64,0},{128,64},{192,128},{1,193},{65,1},{129,65},{193,129... | collective-permute-start | bytes 884744 | tf_op jit(solution)/shard_map/ppermute | solution.py:738
  89.4 27.9 %collective-permute-start.27 = (f32[72,8,128]{2,1,0:T(8,128)S(1)}, f32[72,8,128]{2,1,0:T(8,128)S(1)}, u32[]{:S(2)}, u32[]{:S(2)}) collective-permute-start(f32[72,8,128]{2,1,0:T(8,128)S(1)} %get-tuple-element.78), channel_id=1, source_target_pairs={{0,64},{64,128},{128,192},{192,0},{1,65},{65,129},{129,193},{193,1... | collective-permute-start | bytes 884744 | tf_op jit(solution)/shard_map/ppermute | solution.py:738
  89.4 5.2 %collective-permute-start.28 = (f32[18,8,128]{2,1,0:T(8,128)S(1)}, f32[18,8,128]{2,1,0:T(8,128)S(1)}, u32[]{:S(2)}, u32[]{:S(2)}) collective-permute-start(f32[18,8,128]{2,1,0:T(8,128)S(1)} %get-tuple-element.79), channel_id=1, source_target_pairs={{0,15},{1,0},{2,1},{3,2},{4,3},{5,4},{6,5},{7,6},{8,7},{9,8},{10,9... | collective-permute-start | bytes 221192 | tf_op jit(solution)/shard_map/ppermute | solution.py:738
  91.3 2.9 %collective-permute-start.32 = (f32[8,128]{1,0:T(8,128)S(1)}, f32[8,128]{1,0:T(8,128)S(1)}, u32[]{:S(2)}, u32[]{:S(2)}) collective-permute-start(f32[8,128]{1,0:T(8,128)S(1)} %get-tuple-element.83.own), channel_id=1, source_target_pairs={{0,16},{16,0},{1,17},{17,1},{2,18},{18,2},{3,19},{19,3},{4,20},{20... | collective-permute-start | bytes 12296 | tf_op jit(solution)/shard_map/ppermute | solution.py:750
  93.4 22.0 %collective-permute-start.29 = (f32[18,8,128]{2,1,0:T(8,128)S(1)}, f32[18,8,128]{2,1,0:T(8,128)S(1)}, u32[]{:S(2)}, u32[]{:S(2)}) collective-permute-start(f32[18,8,128]{2,1,0:T(8,128)S(1)} %get-tuple-element.80), channel_id=1, source_target_pairs={{0,1},{1,2},{2,3},{3,4},{4,5},{5,6},{6,7},{7,8},{8,9},{9,10},{10,1... | collective-permute-start | bytes 221192 | tf_op jit(solution)/shard_map/ppermute | solution.py:738
  94.2 23.0 %collective-permute-start.30 = (f32[18,8,128]{2,1,0:T(8,128)S(1)}, f32[18,8,128]{2,1,0:T(8,128)S(1)}, u32[]{:S(2)}, u32[]{:S(2)}) collective-permute-start(f32[18,8,128]{2,1,0:T(8,128)S(1)} %get-tuple-element.81), channel_id=1, source_target_pairs={{0,16},{16,0},{1,17},{17,1},{2,18},{18,2},{3,19},{19,3},{4,20},{20... | collective-permute-start | bytes 221192 | tf_op jit(solution)/shard_map/ppermute | solution.py:750
  94.6 22.7 %collective-permute-start.31 = (f32[18,8,128]{2,1,0:T(8,128)S(1)}, f32[18,8,128]{2,1,0:T(8,128)S(1)}, u32[]{:S(2)}, u32[]{:S(2)}) collective-permute-start(f32[18,8,128]{2,1,0:T(8,128)S(1)} %get-tuple-element.82), channel_id=1, source_target_pairs={{16,32},{48,0},{32,16},{0,48},{17,33},{49,1},{33,17},{1,49},{18,34... | collective-permute-start | bytes 221192 | tf_op jit(solution)/shard_map/ppermute | solution.py:750
  115.4 4.0 %collective-permute-start.33 = (f32[8,128]{1,0:T(8,128)S(1)}, f32[8,128]{1,0:T(8,128)S(1)}, u32[]{:S(2)}, u32[]{:S(2)}) collective-permute-start(f32[8,128]{1,0:T(8,128)S(1)} %shard_map.61.sums), channel_id=1, source_target_pairs={{0,32},{32,0},{1,33},{33,1},{2,34},{34,2},{3,35},{35,3},{4,36},{36... | collective-permute-start | bytes 12296 | tf_op jit(solution)/shard_map/ppermute | solution.py:750
